TPU v7x, 32 devices: a whole 2x2x4 slice. The times are simulated.
32 devices in a mesh: real: 2 (over y), env: 4 (over z), mpo: 2 (over x), col: 2 (over core).
Axes of the slice: x: 2, y: 2, z: 4, core: 2. Of those that a mesh axis runs over, the one named last changes fastest.
Arguments:
- held: bfloat16 [3072, 8, 384], P(('real', 'env', 'col')), parts along dimension 0, may hold values from -0.15625 to 0.15625
- owner_map: int32 [8, 192], P('real'), parts along dimension 0, may hold values from 0 to 1535, as said below
- kept: int32 [8], P(('real', 'env')), parts along dimension 0, may hold values from 96 to 384
- left_env: bfloat16 [14, 8, 384, 384], P('mpo', ('real', 'env')), parts along dimension 1, may hold values from -6 to 6
- mpo_tensor: float32 [14, 14, 4, 4], replicated, may hold values from -1 to 1
- mpo_mask: int32 [14, 14], replicated, may hold values 0 or 1
- fields: float32 [4], P('real'), parts along dimension 0, may hold values from -2 to 2
Outputs:
- new_env: float32 [14, 8, 384, 384], P('mpo', ('real', 'env'), None, 'col'), parts along dimension 1
There are 2 independent parts, one for each index of `real`. A program takes and returns all parts, laid end to end along the dimension named above; an argument that names none is the same for every part. Nothing has to cross between parts.
Inputs may be any that keep to these rules, and one draw needn't show every extreme that they name: owner_map[t, j] is the slot of held that holds tile j of sector t; all entries differ. The owner of index o along env+col holds the slots o * 192 to (o + 1) * 192 - 1. Among the tiles of one sector (the sector of one env index), one owner holds at most 48, and for every sector some owner holds exactly 48.
All inputs are finite; a program needn't handle non-finite values.
Results may differ from a plain program's by a relative error of at most 0.0042.
Values may be sent and summed in bfloat16 or wider, within the bound.
A program may use at most 64 MiB of HBM per device.

v0:
```python
import functools

import jax
import jax.numpy as jnp
from jax import lax
from jax.experimental import pallas as pl
from jax.experimental.pallas import tpu as pltpu
from jax.sharding import PartitionSpec as P

MESH = pl.DeviceIdType.MESH
LANES = 128
GROUP = 4
BF = jnp.bfloat16


def iota(shape, dim):
    return lax.broadcasted_iota(jnp.int32, shape, dim)


def one_hot(condition):
    return jnp.where(condition, jnp.float32(1), jnp.float32(0)).astype(BF)


def mm(a, b):
    return jnp.dot(a, b, preferred_element_type=jnp.float32)


def list_kernel(cores, pool, map_ref, list_ref):
    rows, tiles = map_ref.shape
    low = (lax.axis_index("env") * cores + lax.axis_index("col")) * pool
    batch = 16 if tiles % 16 == 0 else 1

    def sector(t, carry):
        def step(b, count):
            found = [map_ref[t, b * batch + i] - low for i in range(batch)]
            places = [count]
            for slot in found:
                mine = lax.shift_right_logical(~slot & (slot - pool), jnp.int32(31))
                places.append(places[-1] + mine)
            for slot, place in zip(found, places):
                list_ref[t, place] = slot
            return places[-1]

        lax.fori_loop(0, tiles // batch, step, jnp.int32(0))
        return carry

    lax.fori_loop(0, rows, sector, jnp.int32(0))


def quotient(value, divisor, limit):
    for shift in range(8, 31):
        factor = -(-(1 << shift) // divisor)
        if limit * factor < 2**31 and (factor * divisor - (1 << shift)) * limit < 1 << shift:
            return lax.shift_right_logical(value * factor, jnp.int32(shift))
    return lax.div(value, jnp.int32(divisor))


def comm_kernel(
    sizes, list_ref, held_ref, left_ref, arrived_ref, other_ref, pool_ref, pack_ref,
    z_send, z_recv, f_send, f_recv, x_send, x_recv, g_send, g_recv, own_sem, pool_sem,
):
    envs, planes, cores = sizes
    env, plane, core = lax.axis_index("env"), lax.axis_index("mpo"), lax.axis_index("col")
    cap = arrived_ref.shape[1]
    slab = left_ref.shape[0]
    part = left_ref.shape[2] // cores
    mate = lax.rem(core + 1, cores)

    fill = pltpu.make_async_copy(held_ref, pool_ref, pool_sem)
    fill.start()
    barrier = pltpu.get_barrier_semaphore()
    for d in range(1, envs):
        pl.semaphore_signal(
            barrier, inc=1, device_id={"env": lax.rem(env + d, envs)}, device_id_type=MESH
        )
    for d in range(1, planes):
        pl.semaphore_signal(
            barrier, inc=1, device_id={"mpo": lax.rem(plane + d, planes)}, device_id_type=MESH
        )
    pl.semaphore_signal(barrier, inc=1, device_id={"col": mate}, device_id_type=MESH)
    pl.semaphore_wait(barrier, envs + planes - 1)

    def z_copy(d):
        target = lax.rem(env + d, envs)
        return pltpu.make_async_remote_copy(
            src_ref=pack_ref.at[d],
            dst_ref=arrived_ref.at[env * cores + core],
            send_sem=z_send.at[d], recv_sem=z_recv.at[d],
            device_id={"env": target}, device_id_type=MESH,
        )

    def f_copy(d):
        source = lax.rem(env - d + envs, envs)
        block = arrived_ref.at[source * cores + core]
        return pltpu.make_async_remote_copy(
            src_ref=pack_ref.at[0] if d == 0 else block,
            dst_ref=block,
            send_sem=f_send.at[d], recv_sem=f_recv.at[d],
            device_id={"col": mate}, device_id_type=MESH,
        )

    def x_copy(d, w):
        rows = pl.ds(pl.multiple_of(core * part, part), part)
        return pltpu.make_async_remote_copy(
            src_ref=left_ref.at[w, 0, rows],
            dst_ref=other_ref.at[(planes - d - 1) * slab + w, rows],
            send_sem=x_send.at[d, w], recv_sem=x_recv.at[d, w],
            device_id={"mpo": lax.rem(plane + d, planes)}, device_id_type=MESH,
        )

    def g_copy(d, w):
        rows = pl.ds(pl.multiple_of(core * part, part), part)
        piece = other_ref.at[(planes - d - 1) * slab + w, rows]
        return pltpu.make_async_remote_copy(
            src_ref=piece, dst_ref=piece,
            send_sem=g_send.at[d, w], recv_sem=g_recv.at[d, w],
            device_id={"col": mate}, device_id_type=MESH,
        )

    own = pltpu.make_async_copy(
        pack_ref.at[0], arrived_ref.at[env * cores + core], own_sem
    )
    z_order = list(range(envs - 1, 0, -1))
    x_order = [(d, w) for w in range(slab) for d in range(1, planes)]
    for d, w in x_order:
        x_copy(d, w).start()
    fill.wait()

    def gather(d):
        target = lax.rem(env + d, envs)

        def step(p, carry):
            slot = jnp.clip(list_ref[target, p], 0, pool_ref.shape[0] - 1)
            pack_ref[d, p] = pool_ref[slot]
            return carry

        lax.fori_loop(0, cap, step, jnp.int32(0), unroll=8 if cap % 8 == 0 else 1)

    for i, d in enumerate(z_order + [0]):
        gather(d)
        if i:
            z_copy(z_order[i - 1]).start()

    waits = [("z", d, (i + 1) / len(z_order)) for i, d in enumerate(z_order)]
    waits += [("x", item, (i + 1) / len(x_order)) for i, item in enumerate(x_order)]
    own_started = False
    for kind, item, _ in sorted(waits, key=lambda entry: entry[2]):
        if kind == "z":
            z_copy(item).wait_recv()
            f_copy(item).start()
        else:
            x_copy(*item).wait_recv()
            g_copy(*item).start()
        if not own_started:
            own_started = True
            own.start()
            f_copy(0).start()
    own.wait()
    f_copy(0).wait()
    for d in z_order:
        z_copy(d).wait_send()
        f_copy(d).wait()
    for item in x_order:
        x_copy(*item).wait_send()
        g_copy(*item).wait()


def contract_kernel(
    cores, pool, bond, map_ref, kept_ref, fields_ref, arrived_ref, near_ref, far_ref, coupling_ref,
    out_ref, left_ref, other_ref, load_sem, count_ref, tiles_ref, own_ref, turned_ref, first_ref, second_ref,
):
    env, core = lax.axis_index("env"), lax.axis_index("col")
    owners, cap, tile, width = arrived_ref.shape
    tiles = map_ref.shape[1]
    states = tiles * tile // width
    slab = left_ref.shape[0]
    slots = slab + other_ref.shape[0]
    padded = coupling_ref.shape[1] // states
    share = width // cores
    lanes = own_ref.shape[2]

    loads = [
        pltpu.make_async_copy(near_ref, left_ref, load_sem.at[0]),
        pltpu.make_async_copy(far_ref, other_ref, load_sem.at[1]),
    ]
    for load in loads:
        load.start()

    for s in range(owners):
        count_ref[s] = 0

    batch = 16 if tiles % 16 == 0 else 1

    def fetch(b, carry):
        sources = [
            quotient(map_ref[env, b * batch + i], pool, pool * owners) for i in range(batch)
        ]
        ranks = []
        for source in sources:
            ranks.append(count_ref[source])
            count_ref[source] = ranks[-1] + 1
        for i in range(batch):
            at = pl.multiple_of((b * batch + i) * tile, tile)
            tiles_ref[pl.ds(at, tile), :] = arrived_ref[sources[i], ranks[i]].astype(jnp.float32)
        return carry

    lax.fori_loop(0, tiles // batch, fetch, jnp.int32(0))

    kept = kept_ref[0]
    blocks = [
        jnp.where(
            iota((width, width), 1) < kept, tiles_ref[pl.ds(s * width, width), :], 0.0
        ).astype(BF)
        for s in range(states)
    ]

    pick = one_hot(
        (iota((width, lanes), 0) == iota((width, lanes), 1) + core * share)
        & (iota((width, lanes), 1) < share)
    )
    for s in range(states):
        own_ref[s] = mm(blocks[s], pick).astype(BF)

    chunk = 256 // states
    span = chunk * states
    row, col = iota((span, span), 0), iota((span, span), 1)
    unit = states * GROUP
    moved = (
        lax.rem(lax.div(row, GROUP), states) * chunk
        + lax.div(row, unit) * GROUP
        + lax.rem(row, GROUP)
    )
    regroup = one_hot(col == moved)
    for h in range(width // chunk):
        stack = jnp.concatenate(
            [blocks[s][h * chunk : (h + 1) * chunk] for s in range(states)], axis=0
        )
        turned_ref[:, pl.ds(h * span, span)] = mm(regroup, stack).T.astype(BF)

    pairs = slab * states
    tall, wide = pairs * GROUP, states * GROUP * padded
    spread_rows = one_hot(lax.div(iota((tall, pairs), 0), GROUP) == iota((tall, pairs), 1))
    source, target = iota((states * padded, wide), 0), iota((states * padded, wide), 1)
    spread_columns = one_hot(
        (lax.div(source, padded) == lax.div(target, GROUP * padded))
        & (lax.rem(source, padded) == lax.rem(target, padded))
    )
    diagonal = lax.rem(iota((tall, wide), 0), GROUP) == lax.rem(
        lax.div(iota((tall, wide), 1), padded), GROUP
    )
    row, col = iota((pairs, states * padded), 0), iota((pairs, states * padded), 1)
    state, slot = lax.div(col, padded), lax.rem(col, padded)
    first_slot = lax.axis_index("mpo") * slab
    turn = jnp.where(first_slot + slot >= slots, slots, 0)
    corner = (
        (first_slot + lax.div(row, states) == 0)
        & (first_slot + slot - turn == bond - 1)
        & (slot < slots)
        & (lax.rem(row, states) == state)
    )
    onsite = fields_ref[0] * (0.5 - lax.div(state, 2).astype(jnp.float32)) + fields_ref[1] * (
        0.5 - lax.rem(state, 2).astype(jnp.float32)
    )
    coupling = coupling_ref[...] + jnp.where(corner, onsite, 0.0)
    high = coupling.astype(BF)
    low = (coupling - high.astype(jnp.float32)).astype(BF)
    both = []
    for piece in (high, low):
        spread = mm(mm(spread_rows, piece).astype(BF), spread_columns)
        both.append(jnp.where(diagonal, spread, 0.0).astype(BF))
    mixing = jnp.concatenate(both, axis=0)

    step = 16
    block_rows = step * padded
    row, col = iota((block_rows, block_rows), 0), iota((block_rows, block_rows), 1)
    interleave = one_hot(col == lax.rem(row, padded) * step + lax.div(row, padded))
    rows_chunk = first_ref.shape[1] // padded
    per_group = GROUP * padded

    def chunk_step(h, carry):
        pieces = []
        for b in range(rows_chunk // step):
            rows = pl.ds(pl.multiple_of(h * rows_chunk + b * step, step), step)
            stack = [left_ref[w, 0, rows, :] for w in range(slab)]
            stack += [other_ref[w, rows, :] for w in range(slots - slab)]
            if padded > slots:
                stack.append(jnp.zeros(((padded - slots) * step, width), BF))
            pieces.append(mm(interleave, jnp.concatenate(stack, axis=0)).astype(BF))
        environment = jnp.concatenate(pieces, axis=0)
        for s in range(states):
            first_ref[s] = mm(environment, own_ref[s]).astype(BF)
        for g in range(rows_chunk // GROUP):
            operand = jnp.concatenate(
                [first_ref[s, pl.ds(g * per_group, per_group), :] for s in range(states)], axis=0
            )
            mixed = mm(mixing, operand)
            mixed = (mixed[:tall] + mixed[tall:]).astype(BF)
            at = pl.multiple_of(h * (rows_chunk * states) + g * unit, unit)
            for v in range(slab):
                second_ref[v, pl.ds(at, unit), :] = mixed[v * unit : (v + 1) * unit]
        return carry

    for load in loads:
        load.wait()
    lax.fori_loop(0, width // rows_chunk, chunk_step, jnp.int32(0))

    def close(v, carry):
        out_ref[v] = mm(turned_ref[...], second_ref[v]).T[:share]
        return carry

    lax.fori_loop(0, slab, close, jnp.int32(0))


def on_device(held, owner_map, kept, left_env, mpo_tensor, mpo_mask, fields):
    envs, cores, planes = (lax.axis_size(name) for name in ("env", "col", "mpo"))
    plane = lax.axis_index("mpo")
    pool, tile, width = held.shape
    rows, tiles = owner_map.shape
    states = tiles * tile // width
    cap = 2 * kept.shape[0] * tiles // (envs * cores)
    slab = left_env.shape[0]
    slots = slab * planes
    padded = -(-slots // 16) * 16
    share = width // cores
    lanes = -(-share // LANES) * LANES
    smem = pl.BlockSpec(memory_space=pltpu.SMEM)
    vmem = pl.BlockSpec(memory_space=pltpu.VMEM)
    anywhere = pl.BlockSpec(memory_space=pl.ANY)
    dma = pltpu.SemaphoreType.DMA

    slot_list = pl.pallas_call(
        functools.partial(list_kernel, cores, pool),
        out_shape=jax.ShapeDtypeStruct((rows, cap + 1), jnp.int32),
        in_specs=[smem],
        out_specs=smem,
        name="slots",
    )(owner_map)

    arrived, other = pl.pallas_call(
        functools.partial(comm_kernel, (envs, planes, cores)),
        out_shape=[
            jax.ShapeDtypeStruct((envs * cores, cap, tile, width), BF),
            jax.ShapeDtypeStruct((slots - slab, width, width), BF),
        ],
        in_specs=[smem, anywhere, anywhere],
        out_specs=[anywhere, anywhere],
        scratch_shapes=[
            pltpu.VMEM((pool, tile, width), BF),
            pltpu.VMEM((envs, cap, tile, width), BF),
            dma((envs,)), dma((envs,)), dma((envs,)), dma((envs,)),
            dma((planes, slab)), dma((planes, slab)), dma((planes, slab)), dma((planes, slab)),
            dma, dma,
        ],
        compiler_params=pltpu.CompilerParams(collective_id=0, has_side_effects=True),
        name="exchange",
    )(slot_list, held, left_env)

    bond = mpo_tensor.shape[0]
    couplings = mpo_tensor * mpo_mask.astype(jnp.float32)[:, :, None, None]
    couplings = jnp.pad(couplings, ((0, slots - bond), (0, slots - bond), (0, 0), (0, 0)))
    couplings = lax.dynamic_slice_in_dim(couplings, plane * slab, slab, 1)
    couplings = jnp.concatenate([couplings, couplings], axis=0)
    couplings = lax.dynamic_slice_in_dim(couplings, plane * slab, slots, 0)
    couplings = jnp.pad(couplings, ((0, padded - slots), (0, 0), (0, 0), (0, 0)))
    couplings = couplings.transpose(1, 2, 3, 0).reshape(slab * states, states * padded)

    chunk_rows = 64 * padded
    result = pl.pallas_call(
        functools.partial(contract_kernel, cores, pool, bond),
        out_shape=jax.ShapeDtypeStruct((slab, share, width), jnp.float32),
        in_specs=[smem, smem, smem, vmem, anywhere, anywhere, vmem],
        out_specs=vmem,
        scratch_shapes=[
            pltpu.VMEM(left_env.shape, BF),
            pltpu.VMEM((slots - slab, width, width), BF),
            dma((2,)),
            pltpu.SMEM((envs * cores,), jnp.int32),
            pltpu.VMEM((tiles * tile, width), jnp.float32),
            pltpu.VMEM((states, width, lanes), BF),
            pltpu.VMEM((width, tiles * tile), BF),
            pltpu.VMEM((states, chunk_rows, lanes), BF),
            pltpu.VMEM((slab, tiles * tile, lanes), BF),
        ],
        compiler_params=pltpu.CompilerParams(vmem_limit_bytes=62 * 1024 * 1024),
        name="contract",
    )(owner_map, kept, fields, arrived, left_env, other, couplings)
    return jnp.swapaxes(result, 1, 2)[:, None]


def solution(mesh):
    return jax.shard_map(
        on_device,
        mesh=mesh,
        in_specs=(
            P(("real", "env", "col"), None, None),
            P("real", None),
            P(("real", "env")),
            P("mpo", ("real", "env"), None, None),
            P(),
            P(),
            P("real"),
        ),
        out_specs=P("mpo", ("real", "env"), None, "col"),
        check_vma=False,
    )
```

profile of v0, /device:TPU:0, one launch (start us, length us, event | category | flops | bytes accessed | tf_op | source)
XLA Modules:
  0.0 66.5 jit_solution(3558978513942497665)
XLA Ops:
  0.0 0.0 copy-start
  0.7 6.5 %slots.1.list_ref = s32[4,49]{1,0:T(4,128)} custom-call(s32[4,192]{1,0:T(4,128)} %map_ref.3), custom_call_target="tpu_custom_call" | custom-call | tf_op jit(solution)/shard_map/slots/pallas_call | solution.py:331
  7.2 0.7 %convert_element_type.5 = f32[14,14]{1,0:T(8,128)S(1)} convert(s32[14,14]{1,0:T(8,128)} %param.12) | non-fusion elementwise | flops 196 | bytes 1568 | tf_op jit(solution)/shard_map/convert_element_type | solution.py:359
  7.9 0.1 copy.10
  8.1 0.0 copy-done
  8.1 0.1 constant_dynamic-slice_fusion
  8.2 0.2 copy.13
  8.4 0.1 dynamic-slice_maximum_fusion
  8.6 0.7 %reshape.4.coupling_ref = f32[28,64]{1,0:T(8,128)} reshape(f32[7,4,4,16]{3,2,1,0:T(4,128)S(1)} %pad_bitcast_fusion) | data formatting | bytes 14336 | tf_op jit(solution)/shard_map/reshape | solution.py:365
  9.3 35.8 %exchange.1 = (bf16[8,48,8,384]{3,2,1,0:T(8,128)(2,1)}, bf16[7,384,384]{2,1,0:T(8,128)(2,1)}) custom-call(s32[4,49]{1,0:T(4,128)} %slots.1.list_ref, bf16[192,8,384]{2,1,0:T(8,128)(2,1)} %held_ref.1, bf16[7,1,384,384]{3,2,1,0:T(8,128)(2,1)} %near_ref.1), custom_call_target="tpu_custom_call" | custom-call | tf_op jit(solution)/shard_map/exchange/pallas_call | solution.py:339
  45.1 21.4 %contract.1 = f32[7,192,384]{2,1,0:T(8,128)} custom-call(s32[4,192]{1,0:T(4,128)} %map_ref.3, s32[1]{0:T(128)S(6)} %copy.14.kept_ref, f32[2]{0:T(128)} %fields_ref.1, bf16[8,48,8,384]{3,2,1,0:T(8,128)(2,1)} %get-tuple-element.7.arrived_ref, bf16[7,1,384,384]{3,2,1,0:T(8,128)(2,1)} %near_ref.1, bf16[7,384,384]{2,1,0:T(8,128)(2,1)} %get-tuple-element.8.far_ref, ...), custom_call_target="tpu_custom_call" | custom-call | tf_op jit(solution)/shard_map/contract/pallas_call | solution.py:368
  (3 shorter events, 0.0 us)
Async XLA Ops:
  0.0 8.1 %copy-start = (f32[14,14,4,4]{1,3,2,0:T(4,128)S(1)}, f32[14,14,4,4]{1,3,2,0:T(4,128)}, u32[]{:S(2)}) copy-start(f32[14,14,4,4]{1,3,2,0:T(4,128)} %param.11) | copy-start | bytes 37636
where the time goes:
time: 66.8 us; the launch traced here: 66.5 us
  Pallas kernels  63.7 us (95%)
  local copies, waits for them, and re-layouts  1.16 us (2%)
  other arithmetic  0.85 us (1%)
  between operations  0.74 us (1%)
    pallas_call x1, Pallas kernels, on_device(): pl.pallas_call(functools.partial(comm_kernel, (envs, planes, cores)), out...  35.8 us
    pallas_call x1, Pallas kernels, on_device(): pl.pallas_call(functools.partial(contract_kernel, cores, pool, bond), out...  21.4 us
    pallas_call x1, Pallas kernels, on_device(): pl.pallas_call(functools.partial(list_kernel, cores, pool), out_shape=jax...  6.55 us

commit v1 on v0

v1 whole, which is shorter than its diff:
```python
import functools

import jax
import jax.numpy as jnp
from jax import lax
from jax.experimental import pallas as pl
from jax.experimental.pallas import tpu as pltpu
from jax.sharding import PartitionSpec as P

MESH = pl.DeviceIdType.MESH
LANES = 128
GROUP = 4
STEP = 16
ROWS = 64
EARLY = 3
BF = jnp.bfloat16
F32 = jnp.float32


def iota(shape, dim):
    return lax.broadcasted_iota(jnp.int32, shape, dim)


def one_hot(condition):
    return jnp.where(condition, F32(1), F32(0)).astype(BF)


def mm(a, b):
    return jnp.dot(a, b, preferred_element_type=F32)


def mm_nt(a, b):
    return lax.dot_general(a, b, (((1,), (1,)), ((), ())), preferred_element_type=F32)


def partner(env, d):
    out = env
    bit = 1
    while bit <= d:
        if d & bit:
            out = out + bit * (1 - 2 * lax.rem(lax.div(env, jnp.int32(bit)), 2))
        bit *= 2
    return out


def tile_lists(map_ref, env, me, pool, owners, cap):
    rows, tiles = map_ref.shape
    table = map_ref[...]
    if rows < 8:
        table = jnp.concatenate([table] * (8 // rows), axis=0)
    local = (table - me * pool).astype(F32)
    mine = (local >= 0) & (local < pool)
    earlier = one_hot(iota((tiles, tiles), 0) < iota((tiles, tiles), 1))
    rank = mm(jnp.where(mine, F32(1), F32(0)).astype(BF), earlier)
    key = jnp.where(mine, rank, F32(-1))
    places = rows * cap
    spread = one_hot(
        lax.div(iota((places, table.shape[0]), 0), cap) == iota((places, table.shape[0]), 1)
    )
    place = lax.rem(iota((places, tiles), 0), cap).astype(F32)
    chosen = one_hot(mm(spread, key.astype(BF)) == place)
    send = mm_nt(jnp.where(mine, local, F32(0)).astype(BF), chosen)
    send = send.astype(jnp.int32)

    row = map_ref[pl.ds(env, 1), :].astype(F32)
    owner = jnp.floor((row + 0.5) * F32(1.0 / pool))
    holds = iota((owners, tiles), 0).astype(F32) == owner
    ranks = mm(one_hot(holds), earlier)
    at = owner * cap + jnp.sum(jnp.where(holds, ranks, F32(0)), axis=0, keepdims=True)
    return send, at.astype(jnp.int32)


def mixing_matrix(tensor_ref, mask_ref, fields_ref, table_ref, plane, slab, slots, padded):
    bond, states = tensor_ref.shape[0], tensor_ref.shape[1]
    table_ref[...] = jnp.zeros_like(table_ref)
    lane, state = iota((states, bond), 1), iota((states, bond), 0)
    onsite = fields_ref[0] * (0.5 - lax.div(state, 2).astype(F32)) + fields_ref[1] * (
        0.5 - lax.rem(state, 2).astype(F32)
    )
    for w in range(bond):
        mask = mask_ref[pl.ds(w, 1), :].astype(F32)
        for q in range(states):
            block = tensor_ref[w, q] * mask
            if w == bond - 1:
                block = block + jnp.where((lane == 0) & (state == q), onsite, F32(0))
            table_ref[pl.ds((w * states + q) * states, states), :bond] = block
    table = table_ref[...]
    high = table.astype(BF)
    low = (table - high.astype(F32)).astype(BF)

    wide, tall = states * GROUP * padded, slab * states * GROUP
    entries = table.shape[0]
    at, entry = iota((wide, entries), 0), iota((wide, entries), 1)
    slot = lax.rem(at, padded)
    bond_index = plane * slab + slot
    bond_index = jnp.where(bond_index >= slots, bond_index - slots, bond_index)
    base = bond_index * (states * states) + lax.div(at, GROUP * padded)
    row, col = iota((tall, LANES), 0), iota((tall, LANES), 1)
    unit = states * GROUP
    diagonal = lax.rem(iota((tall, wide), 0), GROUP) == lax.rem(
        lax.div(iota((tall, wide), 1), padded), GROUP
    )
    parts = [jnp.zeros((tall, wide), F32), jnp.zeros((tall, wide), F32)]
    for q in range(states):
        source = one_hot((entry == base + q * states) & (slot < slots))
        target = one_hot(
            (lax.div(lax.rem(row, unit), GROUP) == q) & (col == plane * slab + lax.div(row, unit))
        )
        for i, piece in enumerate((high, low)):
            parts[i] = parts[i] + mm_nt(target, mm(source, piece).astype(BF))
    return jnp.concatenate([jnp.where(diagonal, part, F32(0)).astype(BF) for part in parts], axis=0)


def fused_kernel(
    sizes, kept_ref, fields_ref, map_ref, tensor_ref, mask_ref, held_ref, left_ref,
    second_ref, turned_ref,
    pool_ref, pack_ref, arrived_ref, near_ref, far_ref, vlist_ref, list_ref, table_ref,
    tiles_ref, own_ref, first_ref,
    z_send, z_recv, f_send, f_recv, s_send, s_recv, t_send, t_recv,
    x_send, x_recv, g_send, g_recv, local_sem,
):
    envs, planes, cores = sizes
    env, plane, core = lax.axis_index("env"), lax.axis_index("mpo"), lax.axis_index("col")
    pool, tile, width = pool_ref.shape
    rows, tiles = map_ref.shape
    owners = envs * cores
    cap = pack_ref.shape[1]
    states = tiles * tile // width
    slab = left_ref.shape[0]
    slots = slab * planes
    padded = -(-slots // 16) * 16
    share = width // cores
    lanes = own_ref.shape[2]
    mate = lax.rem(core + 1, cores)
    me = env * cores + core
    chunks = width // ROWS
    part = ROWS // cores
    early = min(EARLY, chunks)
    half = cap // planes
    shared = [d >= envs // 2 and cap % planes == 0 for d in range(envs)]

    fill = pltpu.make_async_copy(held_ref, pool_ref, local_sem.at[0])
    fill.start()
    barrier = pltpu.get_barrier_semaphore()
    for d in range(1, envs):
        pl.semaphore_signal(
            barrier, inc=1, device_id={"env": partner(env, d)}, device_id_type=MESH
        )
    for d in range(1, planes):
        pl.semaphore_signal(
            barrier, inc=1, device_id={"mpo": lax.rem(plane + d, planes)}, device_id_type=MESH
        )
    pl.semaphore_signal(barrier, inc=1, device_id={"col": mate}, device_id_type=MESH)

    send, at = tile_lists(map_ref, env, me, pool, owners, cap)
    send_rows = send.shape[0]
    vlist_ref[:send_rows] = send
    vlist_ref[pl.ds(send_rows, 8)] = jnp.broadcast_to(at, (8, tiles))
    lists = pltpu.make_async_copy(vlist_ref, list_ref, local_sem.at[1])
    lists.start()
    near = pltpu.make_async_copy(left_ref, near_ref, local_sem.at[2])
    near.start()
    pl.semaphore_wait(barrier, envs + planes - 1)

    def span(d, owner_plane):
        return (owner_plane * half, half) if shared[d] else (0, cap)

    def z_copy(d):
        start, count = span(d, plane)
        return pltpu.make_async_remote_copy(
            src_ref=pack_ref.at[d - 1, pl.ds(0, count)],
            dst_ref=arrived_ref.at[pl.ds(me * cap + start, count)],
            send_sem=z_send.at[d], recv_sem=z_recv.at[d],
            device_id={"env": partner(env, d)}, device_id_type=MESH,
        )

    def landed(d, owner_plane):
        start, count = (0, cap) if d == 0 else span(d, owner_plane)
        source = (partner(env, d) if d else env) * cores + core
        return arrived_ref.at[pl.ds(source * cap + start, count)]

    def f_copy(d):
        return pltpu.make_async_remote_copy(
            src_ref=landed(d, plane), dst_ref=landed(d, plane),
            send_sem=f_send.at[d], recv_sem=f_recv.at[d],
            device_id={"col": mate}, device_id_type=MESH,
        )

    def s_copy(d, e):
        return pltpu.make_async_remote_copy(
            src_ref=landed(d, plane), dst_ref=landed(d, plane),
            send_sem=s_send.at[d, e], recv_sem=s_recv.at[d, e],
            device_id={"mpo": lax.rem(plane + e, planes)}, device_id_type=MESH,
        )

    def t_copy(d, e):
        block = landed(d, lax.rem(plane + planes - e, planes))
        return pltpu.make_async_remote_copy(
            src_ref=block, dst_ref=block,
            send_sem=t_send.at[d, e], recv_sem=t_recv.at[d, e],
            device_id={"col": mate}, device_id_type=MESH,
        )

    def x_copy(d, h):
        piece = pl.ds(pl.multiple_of(h * ROWS + core * part, part), part)
        return pltpu.make_async_remote_copy(
            src_ref=left_ref.at[:, 0, piece],
            dst_ref=far_ref.at[pl.ds((planes - d - 1) * slab, slab), piece],
            send_sem=x_send.at[d, h], recv_sem=x_recv.at[d, h],
            device_id={"mpo": lax.rem(plane + d, planes)}, device_id_type=MESH,
        )

    def g_copy(d, h):
        piece = pl.ds(pl.multiple_of(h * ROWS + core * part, part), part)
        block = far_ref.at[pl.ds((planes - d - 1) * slab, slab), piece]
        return pltpu.make_async_remote_copy(
            src_ref=block, dst_ref=block,
            send_sem=g_send.at[d, h], recv_sem=g_recv.at[d, h],
            device_id={"col": mate}, device_id_type=MESH,
        )

    def x_start(h):
        for d in range(1, planes):
            x_copy(d, h).start()

    def x_pass(h):
        for d in range(1, planes):
            x_copy(d, h).wait_recv()
            g_copy(d, h).start()

    for h in range(early):
        x_start(h)
    fill.wait()
    lists.wait()

    def gather(count, slot_at, store):
        def step(p, carry):
            store(p, pool_ref[jnp.clip(slot_at(p), 0, pool - 1)])
            return carry

        lax.fori_loop(0, count, step, jnp.int32(0), unroll=8 if count % 8 == 0 else 1)

    z_order = list(range(envs - 1, 0, -1))
    for d in z_order:
        target = partner(env, d)
        start, count = span(d, plane)

        def store(p, value, d=d):
            pack_ref[d - 1, p] = value

        gather(count, lambda p: list_ref[target, target * cap + start + p], store)
        z_copy(d).start()

    def keep(p, value):
        arrived_ref[me * cap + p] = value

    gather(cap, lambda p: list_ref[env, env * cap + p], keep)
    f_copy(0).start()

    mixing = mixing_matrix(
        tensor_ref, mask_ref, fields_ref, table_ref, plane, slab, slots, padded
    )

    for d in z_order:
        z_copy(d).wait_recv()
        if shared[d]:
            for e in range(1, planes):
                s_copy(d, e).start()
        f_copy(d).start()
    for h in range(early, chunks):
        x_start(h)
    for h in range(early):
        x_pass(h)
    for d in z_order:
        if shared[d]:
            for e in range(1, planes):
                s_copy(d, e).wait_recv()
                t_copy(d, e).start()
    for d in range(envs):
        f_copy(d).wait_recv()
    for d in z_order:
        if shared[d]:
            for e in range(1, planes):
                t_copy(d, e).wait_recv()

    batch = 16 if tiles % 16 == 0 else 1

    def fetch(b, carry):
        for i in range(batch):
            j = b * batch + i
            to = pl.multiple_of(j * tile, tile)
            source = jnp.clip(list_ref[send_rows, j], 0, owners * cap - 1)
            tiles_ref[pl.ds(to, tile), :] = arrived_ref[source].astype(F32)
        return carry

    lax.fori_loop(0, tiles // batch, fetch, jnp.int32(0))

    kept = kept_ref[0]
    blocks = [
        jnp.where(
            iota((width, width), 1) < kept, tiles_ref[pl.ds(s * width, width), :], F32(0)
        ).astype(BF)
        for s in range(states)
    ]
    pick = one_hot(
        (iota((width, lanes), 0) == iota((width, lanes), 1) + core * share)
        & (iota((width, lanes), 1) < share)
    )
    for s in range(states):
        own_ref[s] = mm(blocks[s], pick).astype(BF)

    chunk = 256 // states
    wide = chunk * states
    row, col = iota((wide, wide), 0), iota((wide, wide), 1)
    unit = states * GROUP
    moved = (
        lax.rem(lax.div(row, GROUP), states) * chunk
        + lax.div(row, unit) * GROUP
        + lax.rem(row, GROUP)
    )
    regroup = one_hot(col == moved)
    for h in range(width // chunk):
        stack = jnp.concatenate(
            [blocks[s][h * chunk : (h + 1) * chunk] for s in range(states)], axis=0
        )
        turned_ref[:, pl.ds(h * wide, wide)] = mm(regroup, stack).T.astype(BF)

    block_rows = STEP * padded
    row, col = iota((block_rows, block_rows), 0), iota((block_rows, block_rows), 1)
    interleave = one_hot(col == lax.rem(row, padded) * STEP + lax.div(row, padded))
    per_group = GROUP * padded
    tall = slab * states * GROUP

    def chunk_step(h, carry):
        @pl.when(h >= early)
        def _():
            x_pass(h)

        for d in range(1, planes):
            g_copy(d, h).wait_recv()
        pieces = []
        for b in range(ROWS // STEP):
            piece = pl.ds(pl.multiple_of(h * ROWS + b * STEP, STEP), STEP)
            stack = [near_ref[w, 0, piece, :] for w in range(slab)]
            stack += [far_ref[w, piece, :] for w in range(slots - slab)]
            if padded > slots:
                stack.append(jnp.zeros(((padded - slots) * STEP, width), BF))
            pieces.append(mm(interleave, jnp.concatenate(stack, axis=0)).astype(BF))
        environment = jnp.concatenate(pieces, axis=0)
        for s in range(states):
            first_ref[s] = mm(environment, own_ref[s]).astype(BF)
        for g in range(ROWS // GROUP):
            operand = jnp.concatenate(
                [first_ref[s, pl.ds(g * per_group, per_group), :] for s in range(states)], axis=0
            )
            mixed = mm(mixing, operand)
            mixed = (mixed[:tall] + mixed[tall:]).astype(BF)
            to = pl.multiple_of(h * (ROWS * states) + g * unit, unit)
            for v in range(slab):
                second_ref[v, pl.ds(to, unit), :] = mixed[v * unit : (v + 1) * unit]
        return carry

    near.wait()
    lax.fori_loop(0, chunks, chunk_step, jnp.int32(0))

    for d in range(envs):
        if d:
            z_copy(d).wait_send()
        f_copy(d).wait_send()
        if shared[d]:
            for e in range(1, planes):
                s_copy(d, e).wait_send()
                t_copy(d, e).wait_send()

    def drain(h, carry):
        for d in range(1, planes):
            x_copy(d, h).wait_send()
            g_copy(d, h).wait_send()
        return carry

    lax.fori_loop(0, chunks, drain, jnp.int32(0))


def close_kernel(second_ref, turned_ref, out_ref):
    slab, share, _ = out_ref.shape

    def close(v, carry):
        out_ref[v] = mm(turned_ref[...], second_ref[v]).T[:share]
        return carry

    lax.fori_loop(0, slab, close, jnp.int32(0))


def on_device(held, owner_map, kept, left_env, mpo_tensor, mpo_mask, fields):
    envs, cores, planes = (lax.axis_size(name) for name in ("env", "col", "mpo"))
    pool, tile, width = held.shape
    rows, tiles = owner_map.shape
    states = tiles * tile // width
    cap = 2 * kept.shape[0] * tiles // (envs * cores)
    slab = left_env.shape[0]
    slots = slab * planes
    padded = -(-slots // 16) * 16
    share = width // cores
    lanes = -(-share // LANES) * LANES
    chunks = width // ROWS
    bond = mpo_tensor.shape[0]
    list_rows = max(rows, 8) + 8
    smem = pl.BlockSpec(memory_space=pltpu.SMEM)
    vmem = pl.BlockSpec(memory_space=pltpu.VMEM)
    anywhere = pl.BlockSpec(memory_space=pl.ANY)
    dma = pltpu.SemaphoreType.DMA
    assert pool <= 256 and envs & (envs - 1) == 0 and kept.shape[0] == 1

    second, turned = pl.pallas_call(
        functools.partial(fused_kernel, (envs, planes, cores)),
        out_shape=[
            jax.ShapeDtypeStruct((slab, tiles * tile, lanes), BF),
            jax.ShapeDtypeStruct((width, tiles * tile), BF),
        ],
        in_specs=[smem, smem, vmem, vmem, vmem, anywhere, anywhere],
        out_specs=[vmem, vmem],
        scratch_shapes=[
            pltpu.VMEM((pool, tile, width), BF),
            pltpu.VMEM((max(envs - 1, 1), cap, tile, width), BF),
            pltpu.VMEM((envs * cores * cap, tile, width), BF),
            pltpu.VMEM(left_env.shape, BF),
            pltpu.VMEM((slots - slab, width, width), BF),
            pltpu.VMEM((list_rows, tiles), jnp.int32),
            pltpu.SMEM((list_rows, tiles), jnp.int32),
            pltpu.VMEM((bond * states * states, LANES), F32),
            pltpu.VMEM((tiles * tile, width), F32),
            pltpu.VMEM((states, width, lanes), BF),
            pltpu.VMEM((states, ROWS * padded, lanes), BF),
            dma((envs,)), dma((envs,)), dma((envs,)), dma((envs,)),
            dma((envs, planes)), dma((envs, planes)), dma((envs, planes)), dma((envs, planes)),
            dma((planes, chunks)), dma((planes, chunks)),
            dma((planes, chunks)), dma((planes, chunks)),
            dma((3,)),
        ],
        compiler_params=pltpu.CompilerParams(
            collective_id=0, has_side_effects=True, vmem_limit_bytes=62 * 1024 * 1024
        ),
        name="fused",
    )(kept, fields, owner_map, mpo_tensor.transpose(0, 2, 3, 1), mpo_mask, held, left_env)

    result = pl.pallas_call(
        close_kernel,
        out_shape=jax.ShapeDtypeStruct((slab, share, width), F32),
        in_specs=[vmem, vmem],
        out_specs=vmem,
        compiler_params=pltpu.CompilerParams(vmem_limit_bytes=62 * 1024 * 1024),
        name="close",
    )(second, turned)
    return jnp.swapaxes(result, 1, 2)[:, None]


def solution(mesh):
    return jax.shard_map(
        on_device,
        mesh=mesh,
        in_specs=(
            P(("real", "env", "col"), None, None),
            P("real", None),
            P(("real", "env")),
            P("mpo", ("real", "env"), None, None),
            P(),
            P(),
            P("real"),
        ),
        out_specs=P("mpo", ("real", "env"), None, "col"),
        check_vma=False,
    )
```

time: 66.8 us -> 58 us (0.87)
  Pallas kernels: 63.7 us -> 57.1 us
  local copies, waits for them, and re-layouts: 1.16 us -> 0 us
  other arithmetic: 0.85 us -> 0 us
    pallas_call x3 -> x2, Pallas kernels: 63.7 us -> 57.1 us  [the longest x1 49.2 us: on_device(): pl.pallas_call(functools.partial(fused_kernel, (envs, planes, cores)), ou...]
    convert_element_type x1 -> x0, other arithmetic: 0.7 us -> none  [on_device(): couplings = mpo_tensor * mpo_mask.astype(jnp.float32)[:, :, None, None]]
    reshape x1 -> x0, local copies, waits for them, and re-layouts: 0.69 us -> none  [on_device(): couplings.transpose(1, 2, 3, 0).reshape(slab * states, states * padded)]
where the time goes in v1:
time: 58 us; the launch traced here: 57.8 us
  Pallas kernels  57.1 us (98%)
  between operations  0.66 us (1%)
    pallas_call x1, Pallas kernels, on_device(): pl.pallas_call(functools.partial(fused_kernel, (envs, planes, cores)), ou...  49.2 us
    pallas_call x1, Pallas kernels, on_device(): pl.pallas_call(close_kernel, out_shape=jax.ShapeDtypeStruct((slab, share,...  7.99 us

profile of v1, /device:TPU:0, one launch (start us, length us, event | category | flops | bytes accessed | tf_op | source)
XLA Modules:
  0.0 57.8 jit_solution(2454297904221592491)
XLA Ops:
  0.7 49.2 %fused.1 = (bf16[7,1536,256]{2,1,0:T(8,128)(2,1)}, bf16[384,1536]{1,0:T(8,128)(2,1)}) custom-call(s32[1]{0:T(128)S(6)} %copy.9.kept_ref, f32[2]{0:T(128)} %fields_ref.1, s32[4,192]{1,0:T(4,128)} %map_ref.1, f32[14,4,4,14]{3,2,1,0:T(4,128)} %bitcast.6, s32[14,14]{1,0:T(8,128)} %mask_ref.1, bf16[192,8,384]{2,1,0:T(8,128)(2,1)} %held_ref.1, ...), custom_call_target="tpu_custom_call" | custom-call | tf_op jit(solution)/shard_map/fused/pallas_call | solution.py:414
  49.8 8.0 %close.1 = f32[7,192,384]{2,1,0:T(8,128)} custom-call(bf16[7,1536,256]{2,1,0:T(8,128)(2,1)} %get-tuple-element.7.second_ref, bf16[384,1536]{1,0:T(8,128)(2,1)} %get-tuple-element.8.turned_ref), custom_call_target="tpu_custom_call" | custom-call | tf_op jit(solution)/shard_map/close/pallas_call | solution.py:446

commit v2 on v1

v2 whole, which is shorter than its diff:
```python
import functools

import jax
import jax.numpy as jnp
from jax import lax
from jax.experimental import pallas as pl
from jax.experimental.pallas import tpu as pltpu
from jax.sharding import PartitionSpec as P

MESH = pl.DeviceIdType.MESH
LANES = 128
GROUP = 4
STEP = 16
ROWS = 64
EARLY = 2
MIDDLE = 1
WINDOW = 2
PIECES = 2
BF = jnp.bfloat16
F32 = jnp.float32


def iota(shape, dim):
    return lax.broadcasted_iota(jnp.int32, shape, dim)


def one_hot(condition):
    return jnp.where(condition, F32(1), F32(0)).astype(BF)


def mm(a, b):
    return jnp.dot(a, b, preferred_element_type=F32)


def mm_nt(a, b):
    return lax.dot_general(a, b, (((1,), (1,)), ((), ())), preferred_element_type=F32)


def mm_tn(a, b):
    return lax.dot_general(a, b, (((0,), (0,)), ((), ())), preferred_element_type=F32)


def partner(env, d):
    out = env
    bit = 1
    while bit <= d:
        if d & bit:
            out = out + bit * (1 - 2 * lax.rem(lax.div(env, jnp.int32(bit)), 2))
        bit *= 2
    return out


def tile_lists(map_ref, env, me, pool, owners, cap):
    rows, tiles = map_ref.shape
    table = map_ref[...]
    if rows < 8:
        table = jnp.concatenate([table] * (8 // rows), axis=0)
    local = (table - me * pool).astype(F32)
    mine = (local >= 0) & (local < pool)
    earlier = one_hot(iota((tiles, tiles), 0) < iota((tiles, tiles), 1))
    rank = mm(jnp.where(mine, F32(1), F32(0)).astype(BF), earlier)
    key = jnp.where(mine, rank, F32(-1))
    places = rows * cap
    spread = one_hot(
        lax.div(iota((places, table.shape[0]), 0), cap) == iota((places, table.shape[0]), 1)
    )
    place = lax.rem(iota((places, tiles), 0), cap).astype(F32)
    chosen = one_hot(mm(spread, key.astype(BF)) == place)
    send = mm_nt(jnp.where(mine, local, F32(0)).astype(BF), chosen)
    send = send.astype(jnp.int32)

    row = map_ref[pl.ds(env, 1), :].astype(F32)
    owner = jnp.floor((row + 0.5) * F32(1.0 / pool))
    holds = iota((owners, tiles), 0).astype(F32) == owner
    ranks = mm(one_hot(holds), earlier)
    at = owner * cap + jnp.sum(jnp.where(holds, ranks, F32(0)), axis=0, keepdims=True)
    return send, at.astype(jnp.int32)


def mixing_matrix(tensor_ref, mask_ref, fields_ref, table_ref, plane, slab, slots, padded):
    bond, states = tensor_ref.shape[0], tensor_ref.shape[1]
    table_ref[...] = jnp.zeros_like(table_ref)
    lane, state = iota((states, bond), 1), iota((states, bond), 0)
    onsite = fields_ref[0] * (0.5 - lax.div(state, 2).astype(F32)) + fields_ref[1] * (
        0.5 - lax.rem(state, 2).astype(F32)
    )
    for w in range(bond):
        mask = mask_ref[pl.ds(w, 1), :].astype(F32)
        for q in range(states):
            block = tensor_ref[w, q] * mask
            if w == bond - 1:
                block = block + jnp.where((lane == 0) & (state == q), onsite, F32(0))
            table_ref[pl.ds((w * states + q) * states, states), :bond] = block
    table = table_ref[...]
    high = table.astype(BF)
    low = (table - high.astype(F32)).astype(BF)

    wide, tall = states * GROUP * padded, slab * states * GROUP
    entries = table.shape[0]
    at, entry = iota((wide, entries), 0), iota((wide, entries), 1)
    slot = lax.rem(at, padded)
    bond_index = plane * slab + slot
    bond_index = jnp.where(bond_index >= slots, bond_index - slots, bond_index)
    base = bond_index * (states * states) + lax.div(at, GROUP * padded)
    row, col = iota((tall, LANES), 0), iota((tall, LANES), 1)
    unit = states * GROUP
    diagonal = lax.rem(iota((tall, wide), 0), GROUP) == lax.rem(
        lax.div(iota((tall, wide), 1), padded), GROUP
    )
    parts = [jnp.zeros((tall, wide), F32), jnp.zeros((tall, wide), F32)]
    for q in range(states):
        source = one_hot((entry == base + q * states) & (slot < slots))
        target = one_hot(
            (lax.div(lax.rem(row, unit), GROUP) == q) & (col == plane * slab + lax.div(row, unit))
        )
        for i, piece in enumerate((high, low)):
            parts[i] = parts[i] + mm_nt(target, mm(source, piece).astype(BF))
    return jnp.concatenate([jnp.where(diagonal, part, F32(0)).astype(BF) for part in parts], axis=0)


def fused_kernel(
    sizes, kept_ref, fields_ref, map_ref, tensor_ref, mask_ref, held_ref, left_ref,
    out_ref,
    pool_ref, pack_ref, arrived_ref, near_ref, far_ref, vlist_ref, list_ref, table_ref,
    tiles_ref, own_ref, first_ref, second_ref, close_ref, vmap_ref, vtensor_ref, vmask_ref,
    z_send, z_recv, f_send, f_recv, s_send, s_recv, t_send, t_recv,
    x_send, x_recv, g_send, g_recv, local_sem,
):
    envs, planes, cores = sizes
    env, plane, core = lax.axis_index("env"), lax.axis_index("mpo"), lax.axis_index("col")
    pool, tile, width = pool_ref.shape
    rows, tiles = map_ref.shape
    owners = envs * cores
    cap = pack_ref.shape[1]
    states = tiles * tile // width
    slab = left_ref.shape[0]
    slots = slab * planes
    padded = -(-slots // 16) * 16
    share = width // cores
    lanes = own_ref.shape[2]
    mate = lax.rem(core + 1, cores)
    me = env * cores + core
    chunks = width // ROWS
    part = ROWS // cores
    half = cap // planes
    pieces = PIECES if half % PIECES == 0 else 1
    shared = [d >= envs // 2 and cap % planes == 0 for d in range(envs)]
    order = range(envs - 1, 0, -1)
    cross = [(d, k) for d in order if shared[d] for k in range(pieces)]
    local = [(d, 0) for d in order if not shared[d]]
    passed = min(EARLY + MIDDLE, chunks)
    begun = min(passed + WINDOW, chunks)

    barrier = pltpu.get_barrier_semaphore()
    for d in range(1, planes):
        pl.semaphore_signal(
            barrier, inc=1, device_id={"mpo": lax.rem(plane + d, planes)}, device_id_type=MESH
        )
    pl.semaphore_signal(barrier, inc=1, device_id={"col": mate}, device_id_type=MESH)
    for d in range(1, envs):
        pl.semaphore_signal(
            barrier, inc=1, device_id={"env": partner(env, d)}, device_id_type=MESH
        )
    loads = [
        pltpu.make_async_copy(source, target, local_sem.at[i])
        for i, (source, target) in enumerate(
            [
                (map_ref, vmap_ref), (held_ref, pool_ref), (tensor_ref, vtensor_ref),
                (mask_ref, vmask_ref), (left_ref, near_ref), (vlist_ref, list_ref),
            ]
        )
    ]
    for load in loads[:5]:
        load.start()
    loads[0].wait()

    send, at = tile_lists(vmap_ref, env, me, pool, owners, cap)
    send_rows = send.shape[0]
    vlist_ref[:send_rows] = send
    vlist_ref[pl.ds(send_rows, 8)] = jnp.broadcast_to(at, (8, tiles))
    loads[5].start()

    def span(d, k, owner_plane):
        count = half // pieces
        return (owner_plane * half + k * count, count) if shared[d] else (0, cap)

    def landed(d, k, owner_plane):
        start, count = (0, cap) if d == 0 else span(d, k, owner_plane)
        source = (partner(env, d) if d else env) * cores + core
        return arrived_ref.at[pl.ds(source * cap + start, count)]

    def z_copy(d, k):
        start, count = span(d, k, plane)
        return pltpu.make_async_remote_copy(
            src_ref=pack_ref.at[d - 1, pl.ds(k * count, count)],
            dst_ref=arrived_ref.at[pl.ds(me * cap + start, count)],
            send_sem=z_send.at[d, k], recv_sem=z_recv.at[d, k],
            device_id={"env": partner(env, d)}, device_id_type=MESH,
        )

    def f_copy(d, k):
        block = landed(d, k, plane)
        return pltpu.make_async_remote_copy(
            src_ref=block, dst_ref=block,
            send_sem=f_send.at[d, k], recv_sem=f_recv.at[d, k],
            device_id={"col": mate}, device_id_type=MESH,
        )

    def s_copies(d, k):
        block = landed(d, k, plane)
        return [
            pltpu.make_async_remote_copy(
                src_ref=block, dst_ref=block,
                send_sem=s_send.at[d, k, e], recv_sem=s_recv.at[d, k, e],
                device_id={"mpo": lax.rem(plane + e, planes)}, device_id_type=MESH,
            )
            for e in range(1, planes)
        ]

    def t_copies(d, k):
        copies = []
        for e in range(1, planes):
            block = landed(d, k, lax.rem(plane + planes - e, planes))
            copies.append(
                pltpu.make_async_remote_copy(
                    src_ref=block, dst_ref=block,
                    send_sem=t_send.at[d, k, e], recv_sem=t_recv.at[d, k, e],
                    device_id={"col": mate}, device_id_type=MESH,
                )
            )
        return copies

    def x_copies(h):
        piece = pl.ds(pl.multiple_of(h * ROWS + core * part, part), part)
        return [
            pltpu.make_async_remote_copy(
                src_ref=left_ref.at[:, 0, piece],
                dst_ref=far_ref.at[pl.ds((planes - d - 1) * slab, slab), piece],
                send_sem=x_send.at[d, h], recv_sem=x_recv.at[d, h],
                device_id={"mpo": lax.rem(plane + d, planes)}, device_id_type=MESH,
            )
            for d in range(1, planes)
        ]

    def g_copies(h):
        piece = pl.ds(pl.multiple_of(h * ROWS + core * part, part), part)
        copies = []
        for d in range(1, planes):
            block = far_ref.at[pl.ds((planes - d - 1) * slab, slab), piece]
            copies.append(
                pltpu.make_async_remote_copy(
                    src_ref=block, dst_ref=block,
                    send_sem=g_send.at[d, h], recv_sem=g_recv.at[d, h],
                    device_id={"col": mate}, device_id_type=MESH,
                )
            )
        return copies

    def start(copies):
        for copy in copies:
            copy.start()

    def sent(copies):
        for copy in copies:
            copy.wait_send()

    def relay(arrivals, copies):
        for arrival, copy in zip(arrivals, copies):
            arrival.wait_recv()
            copy.start()

    pl.semaphore_wait(barrier, envs + planes - 1)
    for h in range(EARLY):
        start(x_copies(h))
    loads[1].wait()
    loads[5].wait()

    def gather(count, first, store):
        def step(p, carry):
            slot = jnp.clip(list_ref[first[0], first[1] + p], 0, pool - 1)
            store(p, pool_ref[slot])
            return carry

        lax.fori_loop(0, count, step, jnp.int32(0), unroll=8 if count % 8 == 0 else 4 if count % 4 == 0 else 1)

    def pack(d, k):
        target = partner(env, d)
        begin, count = span(d, k, plane)

        def store(p, value):
            pack_ref[d - 1, k * count + p] = value

        gather(count, (target, target * cap + begin), store)

    ahead = cross[:WINDOW] + local
    for item in ahead:
        pack(*item)
        z_copy(*item).start()
    for item in cross[WINDOW:]:
        pack(*item)

    def keep(p, value):
        arrived_ref[me * cap + p] = value

    gather(cap, (env, env * cap), keep)
    f_copy(0, 0).start()

    loads[2].wait()
    loads[3].wait()
    mixing = mixing_matrix(
        vtensor_ref, vmask_ref, fields_ref, table_ref, plane, slab, slots, padded
    )
    out_ref[...] = jnp.zeros_like(out_ref)

    for i, item in enumerate(cross):
        if i + WINDOW < len(cross):
            z_copy(*item).wait_send()
            z_copy(*cross[i + WINDOW]).start()
        z_copy(*item).wait_recv()
        start(s_copies(*item))
        f_copy(*item).start()
        if i == len(cross) // 2 - 1:
            for h in range(EARLY, passed):
                start(x_copies(h))
    if not cross:
        for h in range(EARLY, passed):
            start(x_copies(h))
    for item in local:
        z_copy(*item).wait_recv()
        f_copy(*item).start()
    for h in range(passed):
        relay(x_copies(h), g_copies(h))
    for item in cross:
        sent(s_copies(*item))
    for h in range(passed, begun):
        start(x_copies(h))
    for item in cross:
        relay(s_copies(*item), t_copies(*item))
    for d, k in [(0, 0)] + cross + local:
        f_copy(d, k).wait_recv()
    for item in cross:
        for copy in t_copies(*item):
            copy.wait_recv()

    batch = 16 if tiles % 16 == 0 else 1

    def fetch(b, carry):
        for i in range(batch):
            j = b * batch + i
            to = pl.multiple_of(j * tile, tile)
            source = jnp.clip(list_ref[send_rows, j], 0, owners * cap - 1)
            tiles_ref[pl.ds(to, tile), :] = arrived_ref[source].astype(F32)
        return carry

    lax.fori_loop(0, tiles // batch, fetch, jnp.int32(0))

    kept = kept_ref[0]
    blocks = [
        jnp.where(
            iota((width, width), 1) < kept, tiles_ref[pl.ds(s * width, width), :], F32(0)
        ).astype(BF)
        for s in range(states)
    ]
    pick = one_hot(
        (iota((width, lanes), 0) == iota((width, lanes), 1) + core * share)
        & (iota((width, lanes), 1) < share)
    )
    for s in range(states):
        own_ref[s] = mm(blocks[s], pick).astype(BF)

    wide = ROWS * states
    row, col = iota((wide, wide), 0), iota((wide, wide), 1)
    unit = states * GROUP
    moved = (
        lax.rem(lax.div(row, GROUP), states) * ROWS
        + lax.div(row, unit) * GROUP
        + lax.rem(row, GROUP)
    )
    regroup = one_hot(col == moved)
    for h in range(chunks):
        stack = jnp.concatenate(
            [blocks[s][h * ROWS : (h + 1) * ROWS] for s in range(states)], axis=0
        )
        close_ref[pl.ds(h * wide, wide), :] = mm(regroup, stack).astype(BF)

    block_rows = STEP * padded
    row, col = iota((block_rows, block_rows), 0), iota((block_rows, block_rows), 1)
    interleave = one_hot(col == lax.rem(row, padded) * STEP + lax.div(row, padded))
    per_group = GROUP * padded
    tall = slab * states * GROUP

    def chunk_step(h, carry):
        @pl.when(h + begun < chunks)
        def _():
            sent(x_copies(h + begun - WINDOW))
            start(x_copies(h + begun))

        @pl.when((h + 1 >= passed) & (h + 1 < chunks))
        def _():
            relay(x_copies(h + 1), g_copies(h + 1))

        for copy in g_copies(h):
            copy.wait_recv()
        parts = []
        for b in range(ROWS // STEP):
            piece = pl.ds(pl.multiple_of(h * ROWS + b * STEP, STEP), STEP)
            stack = [near_ref[w, 0, piece, :] for w in range(slab)]
            stack += [far_ref[w, piece, :] for w in range(slots - slab)]
            if padded > slots:
                stack.append(jnp.zeros(((padded - slots) * STEP, width), BF))
            parts.append(mm(interleave, jnp.concatenate(stack, axis=0)).astype(BF))
        environment = jnp.concatenate(parts, axis=0)
        for s in range(states):
            first_ref[s] = mm(environment, own_ref[s]).astype(BF)
        for g in range(ROWS // GROUP):
            operand = jnp.concatenate(
                [first_ref[s, pl.ds(g * per_group, per_group), :] for s in range(states)], axis=0
            )
            mixed = mm(mixing, operand)
            mixed = (mixed[:tall] + mixed[tall:]).astype(BF)
            for v in range(slab):
                second_ref[v, pl.ds(g * unit, unit), :] = mixed[v * unit : (v + 1) * unit]
        right = close_ref[pl.ds(pl.multiple_of(h * wide, wide), wide), :]
        for v in range(slab):
            out_ref[v] += mm_tn(second_ref[v], right)[:share]
        return carry

    loads[4].wait()
    lax.fori_loop(0, chunks, chunk_step, jnp.int32(0))

    for item in cross[max(len(cross) - WINDOW, 0):] + local:
        z_copy(*item).wait_send()
    for d, k in [(0, 0)] + cross + local:
        f_copy(d, k).wait_send()
    for item in cross:
        sent(t_copies(*item))
    waited = range(begun - WINDOW, chunks - WINDOW) if begun < chunks else range(0)
    for h in range(chunks):
        if h not in waited:
            sent(x_copies(h))
        sent(g_copies(h))


def on_device(held, owner_map, kept, left_env, mpo_tensor, mpo_mask, fields):
    envs, cores, planes = (lax.axis_size(name) for name in ("env", "col", "mpo"))
    pool, tile, width = held.shape
    rows, tiles = owner_map.shape
    states = tiles * tile // width
    cap = 2 * kept.shape[0] * tiles // (envs * cores)
    slab = left_env.shape[0]
    slots = slab * planes
    padded = -(-slots // 16) * 16
    share = width // cores
    lanes = -(-share // LANES) * LANES
    chunks = width // ROWS
    bond = mpo_tensor.shape[0]
    list_rows = max(rows, 8) + 8
    smem = pl.BlockSpec(memory_space=pltpu.SMEM)
    vmem = pl.BlockSpec(memory_space=pltpu.VMEM)
    anywhere = pl.BlockSpec(memory_space=pl.ANY)
    dma = pltpu.SemaphoreType.DMA
    assert pool <= 256 and envs & (envs - 1) == 0 and kept.shape[0] == 1

    pieces = PIECES if cap // planes % PIECES == 0 else 1
    result = pl.pallas_call(
        functools.partial(fused_kernel, (envs, planes, cores)),
        out_shape=pltpu.VMEM((slab, share, width), F32),
        in_specs=[smem, smem] + [anywhere] * 5,
        out_specs=vmem,
        scratch_shapes=[
            pltpu.VMEM((pool, tile, width), BF),
            pltpu.VMEM((max(envs - 1, 1), cap, tile, width), BF),
            pltpu.VMEM((envs * cores * cap, tile, width), BF),
            pltpu.VMEM(left_env.shape, BF),
            pltpu.VMEM((slots - slab, width, width), BF),
            pltpu.VMEM((list_rows, tiles), jnp.int32),
            pltpu.SMEM((list_rows, tiles), jnp.int32),
            pltpu.VMEM((bond * states * states, LANES), F32),
            pltpu.VMEM((tiles * tile, width), F32),
            pltpu.VMEM((states, width, lanes), BF),
            pltpu.VMEM((states, ROWS * padded, lanes), BF),
            pltpu.VMEM((slab, ROWS * states, lanes), BF),
            pltpu.VMEM((tiles * tile, width), BF),
            pltpu.VMEM(owner_map.shape, jnp.int32),
            pltpu.VMEM((bond, states, states, bond), F32),
            pltpu.VMEM(mpo_mask.shape, jnp.int32),
            dma((envs, pieces)), dma((envs, pieces)), dma((envs, pieces)), dma((envs, pieces)),
            dma((envs, pieces, planes)), dma((envs, pieces, planes)),
            dma((envs, pieces, planes)), dma((envs, pieces, planes)),
            dma((planes, chunks)), dma((planes, chunks)),
            dma((planes, chunks)), dma((planes, chunks)),
            dma((6,)),
        ],
        compiler_params=pltpu.CompilerParams(
            collective_id=0,
            has_side_effects=True,
            vmem_limit_bytes=62 * 1024 * 1024 - slab * share * width * 4,
        ),
        name="fused",
    )(kept, fields, owner_map, mpo_tensor.transpose(0, 2, 3, 1), mpo_mask, held, left_env)
    return jnp.swapaxes(result, 1, 2)[:, None]


def solution(mesh):
    return jax.shard_map(
        on_device,
        mesh=mesh,
        in_specs=(
            P(("real", "env", "col"), None, None),
            P("real", None),
            P(("real", "env")),
            P("mpo", ("real", "env"), None, None),
            P(),
            P(),
            P("real"),
        ),
        out_specs=P("mpo", ("real", "env"), None, "col"),
        check_vma=False,
    )
```

time: 58 us -> 48.4 us (0.83)
  Pallas kernels: 57.1 us -> 46.2 us
  local copies, waits for them, and re-layouts: 0 us -> 1.31 us
    pallas_call x1 -> x0, Pallas kernels: 7.99 us -> none  [on_device(): pl.pallas_call(close_kernel, out_shape=jax.ShapeDtypeStruct((slab, share,...]
    pallas_call x1, Pallas kernels: 49.2 us -> 46.2 us  [on_device(): pl.pallas_call(functools.partial(fused_kernel, (envs, planes, cores)), ou...]
    unnamed x0 -> x1, local copies, waits for them, and re-layouts: none -> 1.31 us
where the time goes in v2:
time: 48.4 us; the launch traced here: 48.2 us
  Pallas kernels  46.2 us (95%)
  local copies, waits for them, and re-layouts  1.31 us (3%)
  between operations  0.66 us (1%)
    pallas_call x1, Pallas kernels, on_device(): pl.pallas_call(functools.partial(fused_kernel, (envs, planes, cores)), ou...  46.2 us
    unnamed x1, local copies, waits for them, and re-layouts  1.31 us

profile of v2, /device:TPU:0, one launch (start us, length us, event | category | flops | bytes accessed | tf_op | source)
XLA Modules:
  0.0 48.2 jit_solution(18253171201677504068)
XLA Ops:
  0.7 46.2 %fused.1 = f32[7,192,384]{2,1,0:T(8,128)S(1)} custom-call(s32[1]{0:T(128)S(6)} %copy.11.kept_ref, f32[2]{0:T(128)} %fields_ref.1, s32[4,192]{1,0:T(4,128)} %map_ref.1, f32[14,4,4,14]{3,2,1,0:T(4,128)} %bitcast.7, s32[14,14]{1,0:T(8,128)} %mask_ref.1, bf16[192,8,384]{2,1,0:T(8,128)(2,1)} %held_ref.1, bf16[7,1,384,384]{3,2,1,0:T(8,128)(2,1)} %left_ref.1), custom_call_target="tpu_custom_call" | custom-call | tf_op jit(solution)/shard_map/fused/pallas_call | solution.py:465
  46.9 1.3 %copy.10 = f32[7,1,384,192]{2,3,1,0:T(8,128)} copy(f32[7,1,384,192]{2,3,1,0:T(8,128)S(1)} %bitcast.6) | data formatting | bytes 4128768

commit v3 on v2

v3 whole, which is shorter than its diff:
```python
import functools

import jax
import jax.numpy as jnp
from jax import lax
from jax.experimental import pallas as pl
from jax.experimental.pallas import tpu as pltpu
from jax.sharding import PartitionSpec as P

MESH = pl.DeviceIdType.MESH
LANES = 128
GROUP = 4
STEP = 16
ROWS = 64
EARLY = 3
WINDOW = 2
PIECES = 1
LAG = 2
PREPARE = 1
STRIDE = 2
DELAY = 1
SOLO = 12
BF = jnp.bfloat16
F32 = jnp.float32


def iota(shape, dim):
    return lax.broadcasted_iota(jnp.int32, shape, dim)


def divisor(count, most):
    return max(i for i in range(1, most + 1) if count % i == 0)


def one_hot(condition):
    return jnp.where(condition, F32(1), F32(0)).astype(BF)


def mm(a, b):
    return jnp.dot(a, b, preferred_element_type=F32)


def mm_nt(a, b):
    return lax.dot_general(a, b, (((1,), (1,)), ((), ())), preferred_element_type=F32)


def mm_tn(a, b):
    return lax.dot_general(a, b, (((0,), (0,)), ((), ())), preferred_element_type=F32)


def partner(env, d):
    out = env
    bit = 1
    while bit <= d:
        if d & bit:
            out = out + bit * (1 - 2 * lax.rem(lax.div(env, jnp.int32(bit)), 2))
        bit *= 2
    return out


def plan(envs, planes, cap):
    solo = cap * SOLO // 48
    shareable = planes > 1 and (cap - solo) % (planes * PIECES) == 0
    count = (cap - solo) // (planes * PIECES)
    far = [d for d in range(envs - 1, 0, -1) if d >= envs // 2] if shareable else []
    near = [d for d in range(envs - 1, 0, -1) if d not in far]
    cross, local, at = [], [], 0
    for d in far:
        for k in range(PIECES):
            cross.append((d, solo + k * planes * count, count, True, at))
            at += count
    for d in far:
        if solo:
            cross.append((d, 0, solo, False, at))
            at += solo
    for d in near:
        local.append((d, 0, cap, False, at))
        at += cap
    return cross, local, at


def tile_lists(map_ref, env, me, pool, owners, cap):
    rows, tiles = map_ref.shape
    table = map_ref[...]
    if rows < 8:
        table = jnp.concatenate([table] * (8 // rows), axis=0)
    local = (table - me * pool).astype(F32)
    mine = (local >= 0) & (local < pool)
    earlier = one_hot(iota((tiles, tiles), 0) < iota((tiles, tiles), 1))
    rank = mm(jnp.where(mine, F32(1), F32(0)).astype(BF), earlier)
    key = jnp.where(mine, rank, F32(-1))
    places = rows * cap
    spread = one_hot(
        lax.div(iota((places, table.shape[0]), 0), cap) == iota((places, table.shape[0]), 1)
    )
    place = lax.rem(iota((places, tiles), 0), cap).astype(F32)
    chosen = one_hot(mm(spread, key.astype(BF)) == place)
    send = mm_nt(jnp.where(mine, local, F32(0)).astype(BF), chosen)
    send = send.astype(jnp.int32)

    row = map_ref[pl.ds(env, 1), :].astype(F32)
    owner = jnp.floor((row + 0.5) * F32(1.0 / pool))
    holds = iota((owners, tiles), 0).astype(F32) == owner
    ranks = mm(one_hot(holds), earlier)
    at = owner * cap + jnp.sum(jnp.where(holds, ranks, F32(0)), axis=0, keepdims=True)
    return send, at.astype(jnp.int32)


def mixing_matrix(tensor_ref, mask_ref, fields_ref, table_ref, plane, slab, slots, padded):
    bond, states = tensor_ref.shape[0], tensor_ref.shape[1]
    table_ref[...] = jnp.zeros_like(table_ref)
    lane, state = iota((states, bond), 1), iota((states, bond), 0)
    onsite = fields_ref[0] * (0.5 - lax.div(state, 2).astype(F32)) + fields_ref[1] * (
        0.5 - lax.rem(state, 2).astype(F32)
    )
    for w in range(bond):
        mask = mask_ref[pl.ds(w, 1), :].astype(F32)
        for q in range(states):
            block = tensor_ref[w, q] * mask
            if w == bond - 1:
                block = block + jnp.where((lane == 0) & (state == q), onsite, F32(0))
            table_ref[pl.ds((w * states + q) * states, states), :bond] = block
    table = table_ref[...]
    high = table.astype(BF)
    low = (table - high.astype(F32)).astype(BF)

    wide, tall = states * GROUP * padded, slab * states * GROUP
    entries = table.shape[0]
    at, entry = iota((wide, entries), 0), iota((wide, entries), 1)
    slot = lax.rem(at, padded)
    bond_index = plane * slab + slot
    bond_index = jnp.where(bond_index >= slots, bond_index - slots, bond_index)
    base = bond_index * (states * states) + lax.div(at, GROUP * padded)
    row, col = iota((tall, LANES), 0), iota((tall, LANES), 1)
    unit = states * GROUP
    diagonal = lax.rem(iota((tall, wide), 0), GROUP) == lax.rem(
        lax.div(iota((tall, wide), 1), padded), GROUP
    )
    parts = [jnp.zeros((tall, wide), F32), jnp.zeros((tall, wide), F32)]
    for q in range(states):
        source = one_hot((entry == base + q * states) & (slot < slots))
        target = one_hot(
            (lax.div(lax.rem(row, unit), GROUP) == q) & (col == plane * slab + lax.div(row, unit))
        )
        for i, piece in enumerate((high, low)):
            parts[i] = parts[i] + mm_nt(target, mm(source, piece).astype(BF))
    return jnp.concatenate([jnp.where(diagonal, part, F32(0)).astype(BF) for part in parts], axis=0)


def fused_kernel(
    sizes, kept_ref, fields_ref, map_ref, tensor_ref, mask_ref, held_ref, left_ref,
    out_ref,
    pool_ref, pack_ref, arrived_ref, near_ref, far_ref, vlist_ref, list_ref, table_ref,
    tiles_ref, blocks_ref, own_ref, env_ref, first_ref, second_ref, vmap_ref, vtensor_ref, vmask_ref,
    mixing_ref, interleave_ref, regroup_ref,
    z_sem, f_sem, s_sem, x_sem, local_sem,
):
    envs, planes, cores = sizes
    env, plane, core = lax.axis_index("env"), lax.axis_index("mpo"), lax.axis_index("col")
    pool, tile, width = pool_ref.shape
    rows, tiles = map_ref.shape
    owners = envs * cores
    cap = arrived_ref.shape[0] // owners
    states = tiles * tile // width
    slab = left_ref.shape[0]
    slots = slab * planes
    padded = -(-slots // 16) * 16
    share = width // cores
    mate = lax.rem(core + 1, cores)
    me = env * cores + core
    chunks = width // ROWS
    part = ROWS // cores
    cross, local, _ = plan(envs, planes, cap)
    every = [(0, 0, cap, False, 0)] + cross + local
    last = max([i for i, item in enumerate(cross) if item[3]], default=-1)
    begun = min(EARLY + 2, chunks)
    late = {STRIDE * (c - begun) + DELAY: c for c in range(begun, chunks)}

    barrier = pltpu.get_barrier_semaphore()
    for d in range(1, planes):
        pl.semaphore_signal(
            barrier, inc=1, device_id={"mpo": lax.rem(plane + d, planes)}, device_id_type=MESH
        )
    pl.semaphore_signal(barrier, inc=1, device_id={"col": mate}, device_id_type=MESH)
    for d in range(1, envs):
        pl.semaphore_signal(
            barrier, inc=1, device_id={"env": partner(env, d)}, device_id_type=MESH
        )
    loads = [
        pltpu.make_async_copy(source, target, local_sem.at[i])
        for i, (source, target) in enumerate(
            [
                (map_ref, vmap_ref), (held_ref, pool_ref), (tensor_ref, vtensor_ref),
                (mask_ref, vmask_ref), (left_ref, near_ref), (vlist_ref, list_ref),
            ]
        )
    ]
    for load in loads[:5]:
        load.start()
    loads[0].wait()

    send, at = tile_lists(vmap_ref, env, me, pool, owners, cap)
    send_rows = send.shape[0]
    vlist_ref[:send_rows] = send
    vlist_ref[pl.ds(send_rows, 8)] = jnp.broadcast_to(at, (8, tiles))
    loads[5].start()

    def landed(item, owner_plane, source_env):
        d, first, count, both, _ = item
        if both:
            first = first + owner_plane * count
        return arrived_ref.at[pl.ds((source_env * cores + core) * cap + first, count)]

    def z_copy(item):
        d, first, count, both, place = item
        n = every.index(item)
        return pltpu.make_async_remote_copy(
            src_ref=pack_ref.at[pl.ds(place, count)],
            dst_ref=landed(item, plane, env),
            send_sem=z_sem.at[n - 1, 0], recv_sem=z_sem.at[n - 1, 1],
            device_id={"env": partner(env, d)}, device_id_type=MESH,
        )

    def f_copy(item):
        n = every.index(item)
        block = landed(item, plane, partner(env, item[0]))
        return pltpu.make_async_remote_copy(
            src_ref=block, dst_ref=block,
            send_sem=f_sem.at[n, 0], recv_sem=f_sem.at[n, 1],
            device_id={"col": mate}, device_id_type=MESH,
        )

    def s_copies(item):
        n = cross.index(item)
        block = landed(item, plane, partner(env, item[0]))
        return [
            pltpu.make_async_remote_copy(
                src_ref=block, dst_ref=block,
                send_sem=s_sem.at[n, e - 1, 0], recv_sem=s_sem.at[n, e - 1, 1],
                device_id={"mpo": lax.rem(plane + e, planes)}, device_id_type=MESH,
            )
            for e in range(1, planes)
        ]

    def t_copies(item):
        n = cross.index(item)
        copies = []
        for e in range(1, planes):
            block = landed(item, lax.rem(plane + planes - e, planes), partner(env, item[0]))
            copies.append(
                pltpu.make_async_remote_copy(
                    src_ref=block, dst_ref=block,
                    send_sem=s_sem.at[n, e - 1, 2], recv_sem=s_sem.at[n, e - 1, 3],
                    device_id={"col": mate}, device_id_type=MESH,
                )
            )
        return copies

    def x_copies(h):
        piece = pl.ds(pl.multiple_of(h * ROWS + core * part, part), part)
        return [
            pltpu.make_async_remote_copy(
                src_ref=left_ref.at[:, 0, piece],
                dst_ref=far_ref.at[pl.ds((planes - d - 1) * slab, slab), piece],
                send_sem=x_sem.at[d - 1, h, 0], recv_sem=x_sem.at[d - 1, h, 1],
                device_id={"mpo": lax.rem(plane + d, planes)}, device_id_type=MESH,
            )
            for d in range(1, planes)
        ]

    def g_copies(h):
        piece = pl.ds(pl.multiple_of(h * ROWS + core * part, part), part)
        copies = []
        for d in range(1, planes):
            block = far_ref.at[pl.ds((planes - d - 1) * slab, slab), piece]
            copies.append(
                pltpu.make_async_remote_copy(
                    src_ref=block, dst_ref=block,
                    send_sem=x_sem.at[d - 1, h, 2], recv_sem=x_sem.at[d - 1, h, 3],
                    device_id={"col": mate}, device_id_type=MESH,
                )
            )
        return copies

    def start(copies):
        for copy in copies:
            copy.start()

    def sent(copies):
        for copy in copies:
            copy.wait_send()

    def relay(arrivals, copies):
        for arrival, copy in zip(arrivals, copies):
            arrival.wait_recv()
            copy.start()

    pl.semaphore_wait(barrier, envs + planes - 1)
    for h in range(EARLY):
        start(x_copies(h))
    loads[1].wait()
    loads[5].wait()

    def gather(count, first, store):
        def step(p, carry):
            slot = jnp.clip(list_ref[first[0], first[1] + p], 0, pool - 1)
            store(p, pool_ref[slot])
            return carry

        lax.fori_loop(0, count, step, jnp.int32(0), unroll=divisor(count, 24))

    def pack(item):
        d, first, count, both, place = item
        target = partner(env, d)
        if both:
            first = first + plane * count

        def store(p, value):
            pack_ref[place + p] = value

        gather(count, (target, target * cap + first), store)

    for item in cross[:WINDOW] + local:
        pack(item)
        z_copy(item).start()
    for item in cross[WINDOW:]:
        pack(item)

    def keep(p, value):
        arrived_ref[me * cap + p] = value

    gather(cap, (env, env * cap), keep)
    f_copy(every[0]).start()

    loads[2].wait()
    loads[3].wait()
    mixing_ref[...] = mixing_matrix(
        vtensor_ref, vmask_ref, fields_ref, table_ref, plane, slab, slots, padded
    )
    out_ref[...] = jnp.zeros_like(out_ref)
    unit = states * GROUP
    wide = ROWS * states
    row, col = iota((wide, wide), 0), iota((wide, wide), 1)
    moved = (
        lax.rem(lax.div(row, GROUP), states) * ROWS
        + lax.div(row, unit) * GROUP
        + lax.rem(row, GROUP)
    )
    regroup_ref[...] = one_hot(col == moved)
    block_rows = STEP * padded
    row, col = iota((block_rows, block_rows), 0), iota((block_rows, block_rows), 1)
    interleave_ref[...] = one_hot(col == lax.rem(row, padded) * STEP + lax.div(row, padded))
    loads[4].wait()

    def weave(h, slot):
        for b in range(ROWS // STEP):
            piece = pl.ds(pl.multiple_of(h * ROWS + b * STEP, STEP), STEP)
            stack = [near_ref[w, 0, piece, :] for w in range(slab)]
            stack += [far_ref[w, piece, :] for w in range(slots - slab)]
            if padded > slots:
                stack.append(jnp.zeros(((padded - slots) * STEP, width), BF))
            env_ref[slot, pl.ds(b * block_rows, block_rows)] = mm(
                interleave_ref[...], jnp.concatenate(stack, axis=0)
            ).astype(BF)

    def prepare():
        for h in range(EARLY):
            relay(x_copies(h), g_copies(h))
        for h in range(EARLY):
            for copy in g_copies(h):
                copy.wait_recv()
            weave(h, h)

    def share_in(i):
        if 0 <= i < len(cross) and cross[i][3]:
            relay(s_copies(cross[i]), t_copies(cross[i]))

    def middle():
        for item in cross[: last + 1]:
            sent(s_copies(item))
        for h in range(EARLY, min(EARLY + 2, chunks)):
            start(x_copies(h))

    if last < 0:
        middle()
        prepare()
    for i, item in enumerate(cross):
        if i + WINDOW < len(cross):
            z_copy(item).wait_send()
            z_copy(cross[i + WINDOW]).start()
        z_copy(item).wait_recv()
        if item[3]:
            start(s_copies(item))
        f_copy(item).start()
        share_in(i - LAG)
        if i == min(PREPARE, len(cross) - 1):
            prepare()
        if i == last:
            middle()
    for item in local:
        z_copy(item).wait_recv()
        f_copy(item).start()
    for i in range(max(len(cross) - LAG, 0), len(cross)):
        share_in(i)
    for item in every:
        f_copy(item).wait_recv()
    for item in cross[: last + 1]:
        for copy in t_copies(item):
            copy.wait_recv()

    batch = divisor(tiles, 64)

    def fetch(b, carry):
        for i in range(batch):
            j = b * batch + i
            to = pl.multiple_of(j * tile, tile)
            source = jnp.clip(list_ref[send_rows, j], 0, owners * cap - 1)
            tiles_ref[pl.ds(to, tile), :] = arrived_ref[source].astype(F32)
        return carry

    lax.fori_loop(0, tiles // batch, fetch, jnp.int32(0))

    kept = kept_ref[0]
    first_lane = core * (width - LANES)
    rest = share - LANES
    lane = iota((width, LANES), 1)
    for s in range(states):
        at_rows = pl.ds(s * width, width)
        whole = tiles_ref[at_rows, :]
        blocks_ref[s] = jnp.where(iota((width, width), 1) < kept, whole, F32(0)).astype(BF)
        main = tiles_ref[at_rows, pl.ds(pl.multiple_of(first_lane, LANES), LANES)]
        main = jnp.where(lane + first_lane < kept, main, F32(0))
        own_ref[:, s * LANES : (s + 1) * LANES] = main.astype(BF)
    for p in range(states // 2):
        middles = [
            jnp.where(
                lane + LANES < kept,
                tiles_ref[pl.ds((2 * p + i) * width, width), LANES : 2 * LANES],
                F32(0),
            )
            for i in range(2)
        ]
        left = jnp.where(core == 0, middles[0], pltpu.roll(middles[0], rest, 1))
        right = jnp.where(core == 0, pltpu.roll(middles[1], rest, 1), middles[1])
        at_lanes = (states + p) * LANES
        own_ref[:, at_lanes : at_lanes + LANES] = jnp.where(lane < rest, left, right).astype(BF)

    per_group = GROUP * padded
    tall = slab * states * GROUP
    span = states * per_group
    groups = ROWS // GROUP
    pairs = -(-slab // 2)
    main_rows = pl.ds(pl.multiple_of(core * rest, rest), LANES)
    rest_rows = pl.ds(pl.multiple_of((1 - core) * LANES, rest), rest)

    def mix(operand):
        mixed = mm(mixing_ref[...], operand)
        return mixed[:tall] + mixed[tall:]

    def halves(even, odd):
        low = iota(even.shape, 1) < rest
        return (
            jnp.where(low, even, pltpu.roll(odd, rest, 1)),
            jnp.where(low, pltpu.roll(even, rest, 1), odd),
        )

    def chunk_step(h, carry):
        for when, c in late.items():

            @pl.when(h == when)
            def _(c=c):
                sent(x_copies(c - WINDOW))
                start(x_copies(c))

        @pl.when((h + 1 >= EARLY) & (h + 1 < chunks))
        def _():
            relay(x_copies(h + 1), g_copies(h + 1))


        @pl.when(h >= EARLY)
        def _():
            for copy in g_copies(h):
                copy.wait_recv()
            weave(h, EARLY)

        slot = jnp.minimum(h, EARLY)
        for g in range(0, groups, 2):
            rows_at = pl.ds(g * per_group, 2 * per_group)
            result = mm(env_ref[slot, rows_at], own_ref[...])
            for i in range(2):
                for s in range(states):
                    first_ref[
                        pl.ds((g + i) * span + s * per_group, per_group), :LANES
                    ] = result[i * per_group : (i + 1) * per_group, s * LANES : (s + 1) * LANES].astype(BF)
            for p in range(states // 2):
                at_lanes = (states + p) * LANES
                pair = result[:, at_lanes : at_lanes + LANES]
                for i, piece in enumerate(halves(pair[:per_group], pair[per_group:])):
                    first_ref[
                        pl.ds(g // 2 * span + (2 * p + i) * per_group, per_group), LANES:
                    ] = piece.astype(BF)
        for g in range(0, groups, 2):
            operand = jnp.concatenate(
                [first_ref[pl.ds((g + i) * span, span), :LANES] for i in range(2)], axis=1
            )
            mixed = mix(operand).astype(BF)
            for i in range(2):
                for v in range(slab):
                    second_ref[pl.ds((g + i) * unit, unit), v * LANES : (v + 1) * LANES] = mixed[
                        v * unit : (v + 1) * unit, i * LANES : (i + 1) * LANES
                    ]
        for g in range(0, groups, 4):
            operand = jnp.concatenate(
                [first_ref[pl.ds((g // 2 + i) * span, span), LANES:] for i in range(2)], axis=1
            )
            mixed = mix(operand)
            for i in range(2):
                for p in range(pairs):
                    both = [
                        mixed[
                            min(2 * p + j, slab - 1) * unit : (min(2 * p + j, slab - 1) + 1) * unit,
                            i * LANES : (i + 1) * LANES,
                        ]
                        for j in range(2)
                    ]
                    for j, piece in enumerate(halves(*both)):
                        second_ref[
                            pl.ds((g + 2 * i + j) * unit, unit),
                            (slab + p) * LANES : (slab + p + 1) * LANES,
                        ] = piece.astype(BF)
        stack = jnp.concatenate(
            [blocks_ref[s, pl.ds(pl.multiple_of(h * ROWS, ROWS), ROWS), :] for s in range(states)],
            axis=0,
        )
        right = mm(regroup_ref[...], stack).astype(BF)
        for v in range(slab):
            out_ref[v, main_rows] += mm_tn(second_ref[:, v * LANES : (v + 1) * LANES], right)
        for p in range(pairs):
            at_lanes = (slab + p) * LANES
            closed = mm_tn(second_ref[:, at_lanes : at_lanes + LANES], right)
            out_ref[2 * p, rest_rows] += closed[:rest]
            if 2 * p + 1 < slab:
                out_ref[2 * p + 1, rest_rows] += closed[rest:]
        return carry

    lax.fori_loop(0, chunks, chunk_step, jnp.int32(0))

    for item in cross[max(len(cross) - WINDOW, 0):] + local:
        z_copy(item).wait_send()
    for item in every:
        f_copy(item).wait_send()
    for item in cross[: last + 1]:
        sent(t_copies(item))
    waited = [c - WINDOW for c in late.values()]
    for h in range(chunks):
        if h not in waited:
            sent(x_copies(h))
        sent(g_copies(h))


def on_device(held, owner_map, kept, left_env, mpo_tensor, mpo_mask, fields):
    envs, cores, planes = (lax.axis_size(name) for name in ("env", "col", "mpo"))
    pool, tile, width = held.shape
    rows, tiles = owner_map.shape
    states = tiles * tile // width
    cap = 2 * kept.shape[0] * tiles // (envs * cores)
    slab = left_env.shape[0]
    slots = slab * planes
    padded = -(-slots // 16) * 16
    share = width // cores
    chunks = width // ROWS
    bond = mpo_tensor.shape[0]
    list_rows = max(rows, 8) + 8
    smem = pl.BlockSpec(memory_space=pltpu.SMEM)
    vmem = pl.BlockSpec(memory_space=pltpu.VMEM)
    anywhere = pl.BlockSpec(memory_space=pl.ANY)
    dma = pltpu.SemaphoreType.DMA
    assert share * 2 == 3 * LANES and width == 3 * LANES and pool <= 256 and envs & (envs - 1) == 0 and kept.shape[0] == 1

    cross, local, packed = plan(envs, planes, cap)
    result = pl.pallas_call(
        functools.partial(fused_kernel, (envs, planes, cores)),
        out_shape=pltpu.VMEM((slab, share, width), F32),
        in_specs=[smem, smem] + [anywhere] * 5,
        out_specs=vmem,
        scratch_shapes=[
            pltpu.VMEM((pool, tile, width), BF),
            pltpu.VMEM((packed, tile, width), BF),
            pltpu.VMEM((envs * cores * cap, tile, width), BF),
            pltpu.VMEM(left_env.shape, BF),
            pltpu.VMEM((slots - slab, width, width), BF),
            pltpu.VMEM((list_rows, tiles), jnp.int32),
            pltpu.SMEM((list_rows, tiles), jnp.int32),
            pltpu.VMEM((bond * states * states, LANES), F32),
            pltpu.VMEM((tiles * tile, width), F32),
            pltpu.VMEM((states, width, width), BF),
            pltpu.VMEM((width, states // 2 * 3 * LANES), BF),
            pltpu.VMEM((EARLY + 1, ROWS * padded, width), BF),
            pltpu.VMEM((ROWS * padded * states, 2 * LANES), BF),
            pltpu.VMEM((ROWS * states, (slab + -(-slab // 2)) * LANES), BF),
            pltpu.VMEM(owner_map.shape, jnp.int32),
            pltpu.VMEM((bond, states, states, bond), F32),
            pltpu.VMEM(mpo_mask.shape, jnp.int32),
            pltpu.VMEM((2 * slab * states * GROUP, states * GROUP * padded), BF),
            pltpu.VMEM((STEP * padded, STEP * padded), BF),
            pltpu.VMEM((ROWS * states, ROWS * states), BF),
            dma((len(cross + local), 2)),
            dma((len(cross + local) + 1, 2)),
            dma((max(sum(item[3] for item in cross), 1), max(planes - 1, 1), 4)),
            dma((max(planes - 1, 1), chunks, 4)),
            dma((6,)),
        ],
        compiler_params=pltpu.CompilerParams(
            collective_id=0,
            has_side_effects=True,
            vmem_limit_bytes=62 * 1024 * 1024 - slab * share * width * 4,
        ),
        name="fused",
    )(kept, fields, owner_map, mpo_tensor.transpose(0, 2, 3, 1), mpo_mask, held, left_env)
    return jnp.swapaxes(result, 1, 2)[:, None]


def solution(mesh):
    return jax.shard_map(
        on_device,
        mesh=mesh,
        in_specs=(
            P(("real", "env", "col"), None, None),
            P("real", None),
            P(("real", "env")),
            P("mpo", ("real", "env"), None, None),
            P(),
            P(),
            P("real"),
        ),
        out_specs=P("mpo", ("real", "env"), None, "col"),
        check_vma=False,
    )
```

time: 48.4 us -> 42.7 us (0.88)
  Pallas kernels: 46.2 us -> 40.3 us
    pallas_call x1, Pallas kernels: 46.2 us -> 40.3 us  [on_device(): pl.pallas_call(functools.partial(fused_kernel, (envs, planes, cores)), ou...]
where the time goes in v3:
time: 42.7 us; the launch traced here: 42.2 us
  Pallas kernels  40.3 us (94%)
  local copies, waits for them, and re-layouts  1.31 us (3%)
  between operations  0.66 us (2%)
    pallas_call x1, Pallas kernels, on_device(): pl.pallas_call(functools.partial(fused_kernel, (envs, planes, cores)), ou...  40.3 us
    unnamed x1, local copies, waits for them, and re-layouts  1.31 us

profile of v3, /device:TPU:0, one launch (start us, length us, event | category | flops | bytes accessed | tf_op | source)
XLA Modules:
  0.0 42.2 jit_solution(17545822436913921759)
XLA Ops:
  0.7 40.3 %fused.1 = f32[7,192,384]{2,1,0:T(8,128)S(1)} custom-call(s32[1]{0:T(128)S(6)} %copy.11.kept_ref, f32[2]{0:T(128)} %fields_ref.1, s32[4,192]{1,0:T(4,128)} %map_ref.1, f32[14,4,4,14]{3,2,1,0:T(4,128)} %bitcast.7, s32[14,14]{1,0:T(8,128)} %mask_ref.1, bf16[192,8,384]{2,1,0:T(8,128)(2,1)} %held_ref.1, bf16[7,1,384,384]{3,2,1,0:T(8,128)(2,1)} %left_ref.1), custom_call_target="tpu_custom_call" | custom-call | tf_op jit(solution)/shard_map/fused/pallas_call | solution.py:581
  40.9 1.3 %copy.10 = f32[7,1,384,192]{2,3,1,0:T(8,128)} copy(f32[7,1,384,192]{2,3,1,0:T(8,128)S(1)} %bitcast.6) | data formatting | bytes 4128768

commit v4 on v3

--- a/solution.py
+++ b/solution.py
@@ -18,7 +18,9 @@
 LAG = 2
 PREPARE = 1
 STRIDE = 2
-DELAY = 1
+DELAY = 0
+BEGUN = 1
+HERE = True
 SOLO = 12
 BF = jnp.bfloat16
 F32 = jnp.float32
@@ -79,7 +81,7 @@
     return cross, local, at
 
 
-def tile_lists(map_ref, env, me, pool, owners, cap):
+def tile_lists(map_ref, me, pool, cap):
     rows, tiles = map_ref.shape
     table = map_ref[...]
     if rows < 8:
@@ -96,14 +98,17 @@
     place = lax.rem(iota((places, tiles), 0), cap).astype(F32)
     chosen = one_hot(mm(spread, key.astype(BF)) == place)
     send = mm_nt(jnp.where(mine, local, F32(0)).astype(BF), chosen)
-    send = send.astype(jnp.int32)
-
+    return send.astype(jnp.int32), earlier
+
+
+def arrivals(map_ref, env, earlier, pool, owners, cap):
+    tiles = map_ref.shape[1]
     row = map_ref[pl.ds(env, 1), :].astype(F32)
     owner = jnp.floor((row + 0.5) * F32(1.0 / pool))
     holds = iota((owners, tiles), 0).astype(F32) == owner
     ranks = mm(one_hot(holds), earlier)
     at = owner * cap + jnp.sum(jnp.where(holds, ranks, F32(0)), axis=0, keepdims=True)
-    return send, at.astype(jnp.int32)
+    return at.astype(jnp.int32)
 
 
 def mixing_matrix(tensor_ref, mask_ref, fields_ref, table_ref, plane, slab, slots, padded):
@@ -150,7 +155,7 @@
 def fused_kernel(
     sizes, kept_ref, fields_ref, map_ref, tensor_ref, mask_ref, held_ref, left_ref,
     out_ref,
-    pool_ref, pack_ref, arrived_ref, near_ref, far_ref, vlist_ref, list_ref, table_ref,
+    pool_ref, pack_ref, arrived_ref, near_ref, far_ref, vlist_ref, list_ref, vsource_ref, source_ref, table_ref,
     tiles_ref, blocks_ref, own_ref, env_ref, first_ref, second_ref, vmap_ref, vtensor_ref, vmask_ref,
     mixing_ref, interleave_ref, regroup_ref,
     z_sem, f_sem, s_sem, x_sem, local_sem,
@@ -173,7 +178,7 @@
     cross, local, _ = plan(envs, planes, cap)
     every = [(0, 0, cap, False, 0)] + cross + local
     last = max([i for i, item in enumerate(cross) if item[3]], default=-1)
-    begun = min(EARLY + 2, chunks)
+    begun = min(EARLY + BEGUN, chunks)
     late = {STRIDE * (c - begun) + DELAY: c for c in range(begun, chunks)}
 
     barrier = pltpu.get_barrier_semaphore()
@@ -192,6 +197,7 @@
             [
                 (map_ref, vmap_ref), (held_ref, pool_ref), (tensor_ref, vtensor_ref),
                 (mask_ref, vmask_ref), (left_ref, near_ref), (vlist_ref, list_ref),
+                (vsource_ref, source_ref),
             ]
         )
     ]
@@ -199,11 +205,14 @@
         load.start()
     loads[0].wait()
 
-    send, at = tile_lists(vmap_ref, env, me, pool, owners, cap)
+    send, earlier = tile_lists(vmap_ref, me, pool, cap)
     send_rows = send.shape[0]
     vlist_ref[:send_rows] = send
-    vlist_ref[pl.ds(send_rows, 8)] = jnp.broadcast_to(at, (8, tiles))
     loads[5].start()
+    vsource_ref[...] = jnp.broadcast_to(
+        arrivals(vmap_ref, env, earlier, pool, owners, cap), (8, tiles)
+    )
+    loads[6].start()
 
     def landed(item, owner_plane, source_env):
         d, first, count, both, _ = item
@@ -334,6 +343,7 @@
 
     loads[2].wait()
     loads[3].wait()
+    loads[6].wait()
     mixing_ref[...] = mixing_matrix(
         vtensor_ref, vmask_ref, fields_ref, table_ref, plane, slab, slots, padded
     )
@@ -375,10 +385,15 @@
         if 0 <= i < len(cross) and cross[i][3]:
             relay(s_copies(cross[i]), t_copies(cross[i]))
 
+    def near_in():
+        for item in local:
+            z_copy(item).wait_recv()
+            f_copy(item).start()
+
     def middle():
         for item in cross[: last + 1]:
             sent(s_copies(item))
-        for h in range(EARLY, min(EARLY + 2, chunks)):
+        for h in range(EARLY, begun):
             start(x_copies(h))
 
     if last < 0:
@@ -397,9 +412,10 @@
             prepare()
         if i == last:
             middle()
-    for item in local:
-        z_copy(item).wait_recv()
-        f_copy(item).start()
+            if HERE:
+                near_in()
+    if last < 0 or not HERE:
+        near_in()
     for i in range(max(len(cross) - LAG, 0), len(cross)):
         share_in(i)
     for item in every:
@@ -414,7 +430,7 @@
         for i in range(batch):
             j = b * batch + i
             to = pl.multiple_of(j * tile, tile)
-            source = jnp.clip(list_ref[send_rows, j], 0, owners * cap - 1)
+            source = jnp.clip(source_ref[0, j], 0, owners * cap - 1)
             tiles_ref[pl.ds(to, tile), :] = arrived_ref[source].astype(F32)
         return carry
 
@@ -467,23 +483,19 @@
     def chunk_step(h, carry):
         for when, c in late.items():
 
-            @pl.when(h == when)
-            def _(c=c):
-                sent(x_copies(c - WINDOW))
+            if h == when:
                 start(x_copies(c))
 
-        @pl.when((h + 1 >= EARLY) & (h + 1 < chunks))
-        def _():
+        if EARLY <= h + 1 < chunks:
             relay(x_copies(h + 1), g_copies(h + 1))
 
 
-        @pl.when(h >= EARLY)
-        def _():
+        if h >= EARLY:
             for copy in g_copies(h):
                 copy.wait_recv()
             weave(h, EARLY)
 
-        slot = jnp.minimum(h, EARLY)
+        slot = min(h, EARLY)
         for g in range(0, groups, 2):
             rows_at = pl.ds(g * per_group, 2 * per_group)
             result = mm(env_ref[slot, rows_at], own_ref[...])
@@ -543,7 +555,8 @@
                 out_ref[2 * p + 1, rest_rows] += closed[rest:]
         return carry
 
-    lax.fori_loop(0, chunks, chunk_step, jnp.int32(0))
+    for h in range(chunks):
+        chunk_step(h, 0)
 
     for item in cross[max(len(cross) - WINDOW, 0):] + local:
         z_copy(item).wait_send()
@@ -551,10 +564,8 @@
         f_copy(item).wait_send()
     for item in cross[: last + 1]:
         sent(t_copies(item))
-    waited = [c - WINDOW for c in late.values()]
     for h in range(chunks):
-        if h not in waited:
-            sent(x_copies(h))
+        sent(x_copies(h))
         sent(g_copies(h))
 
 
@@ -570,7 +581,7 @@
     share = width // cores
     chunks = width // ROWS
     bond = mpo_tensor.shape[0]
-    list_rows = max(rows, 8) + 8
+    list_rows = max(rows, 8)
     smem = pl.BlockSpec(memory_space=pltpu.SMEM)
     vmem = pl.BlockSpec(memory_space=pltpu.VMEM)
     anywhere = pl.BlockSpec(memory_space=pl.ANY)
@@ -591,6 +602,8 @@
             pltpu.VMEM((slots - slab, width, width), BF),
             pltpu.VMEM((list_rows, tiles), jnp.int32),
             pltpu.SMEM((list_rows, tiles), jnp.int32),
+            pltpu.VMEM((8, tiles), jnp.int32),
+            pltpu.SMEM((8, tiles), jnp.int32),
             pltpu.VMEM((bond * states * states, LANES), F32),
             pltpu.VMEM((tiles * tile, width), F32),
             pltpu.VMEM((states, width, width), BF),
@@ -608,7 +621,7 @@
             dma((len(cross + local) + 1, 2)),
             dma((max(sum(item[3] for item in cross), 1), max(planes - 1, 1), 4)),
             dma((max(planes - 1, 1), chunks, 4)),
-            dma((6,)),
+            dma((7,)),
         ],
         compiler_params=pltpu.CompilerParams(
             collective_id=0,

time: 42.7 us -> 41.8 us (0.979)
  Pallas kernels: 40.3 us -> 39.6 us
    pallas_call x1, Pallas kernels: 40.3 us -> 39.6 us  [on_device(): pl.pallas_call(functools.partial(fused_kernel, (envs, planes, cores)), ou...]
where the time goes in v4:
time: 41.8 us; the launch traced here: 41.5 us
  Pallas kernels  39.6 us (95%)
  local copies, waits for them, and re-layouts  1.31 us (3%)
  between operations  0.66 us (2%)
    pallas_call x1, Pallas kernels, on_device(): pl.pallas_call(functools.partial(fused_kernel, (envs, planes, cores)), ou...  39.6 us
    unnamed x1, local copies, waits for them, and re-layouts  1.31 us

profile of v4, /device:TPU:0, one launch (start us, length us, event | category | flops | bytes accessed | tf_op | source)
XLA Modules:
  0.0 41.5 jit_solution(3084266210509436348)
XLA Ops:
  0.7 39.6 %fused.1 = f32[7,192,384]{2,1,0:T(8,128)S(1)} custom-call(s32[1]{0:T(128)S(6)} %copy.11.kept_ref, f32[2]{0:T(128)} %fields_ref.1, s32[4,192]{1,0:T(4,128)} %map_ref.1, f32[14,4,4,14]{3,2,1,0:T(4,128)} %bitcast.7, s32[14,14]{1,0:T(8,128)} %mask_ref.1, bf16[192,8,384]{2,1,0:T(8,128)(2,1)} %held_ref.1, bf16[7,1,384,384]{3,2,1,0:T(8,128)(2,1)} %left_ref.1), custom_call_target="tpu_custom_call" | custom-call | tf_op jit(solution)/shard_map/fused/pallas_call | solution.py:592
  40.2 1.3 %copy.10 = f32[7,1,384,192]{2,3,1,0:T(8,128)} copy(f32[7,1,384,192]{2,3,1,0:T(8,128)S(1)} %bitcast.6) | data formatting | bytes 4128768
